TPU v7x, 8 devices: a whole 2x2x1 slice. The times are simulated.
8 devices in a mesh: dp: 2 (over z, y), tp: 4 (over x, core).
Axes of the slice: x: 2, y: 2, z: 1, core: 2. Of those that a mesh axis runs over, the one named last changes fastest.
Arguments:
- hidden: bfloat16 [6, 64, 4096], P('dp', 'tp'), parts along dimension 0
- ln1_gain: float32 [4096], replicated
- ln1_bias: float32 [4096], replicated
- w_qkv: bfloat16 [4096, 3, 32, 128], P(None, None, 'tp')
- b_qkv: bfloat16 [3, 32, 128], P(None, 'tp')
- w_out: bfloat16 [32, 128, 4096], P('tp')
- b_out: bfloat16 [4096], replicated
- ln2_gain: float32 [4096], replicated
- ln2_bias: float32 [4096], replicated
- w_up: bfloat16 [4096, 16384], P(None, 'tp')
- b_up: bfloat16 [16384], P('tp')
- w_down: bfloat16 [16384, 4096], P('tp')
- b_down: bfloat16 [4096], replicated
Outputs:
- output: bfloat16 [6, 64, 4096], P('dp', 'tp'), parts along dimension 0
There are 2 independent parts. A program takes and returns all parts, laid end to end along the dimension named above; an argument that names none is the same for every part.
All inputs are finite; a program needn't handle non-finite values.
Results may differ from a plain program's by a relative error of at most 0.010159.
Values are sent between devices in bfloat16 or wider.
A program may use at most 1 GiB of HBM per device.

v0:
```python
import jax
import jax.numpy as jnp
from jax import lax
from jax.sharding import PartitionSpec as P

LN_EPS = 1e-5


def layer_norm(inputs, gain_vec, shift_vec):
    as_f32 = inputs.astype(jnp.float32)
    row_mean = jnp.mean(as_f32, axis=-1, keepdims=True)
    centered = as_f32 - row_mean
    variance = jnp.mean(centered * centered, axis=-1, keepdims=True)
    return (centered * lax.rsqrt(variance + LN_EPS) * gain_vec + shift_vec).astype(jnp.bfloat16)


def causal_attention(queries, keys_all, values):
    seq_len = queries.shape[1]
    head_dim = queries.shape[3]
    logits = jnp.einsum("bqhd,bkhd->bhqk", queries, keys_all, preferred_element_type=jnp.float32) * head_dim ** -0.5
    causal = lax.broadcasted_iota(jnp.int32, (seq_len, seq_len), 0) >= lax.broadcasted_iota(jnp.int32, (seq_len, seq_len), 1)
    logits = jnp.where(causal, logits, -1e30)
    row_max = jnp.max(logits, axis=-1, keepdims=True)
    exp_vals = jnp.exp(logits - row_max)
    weights_bf = (exp_vals / jnp.sum(exp_vals, axis=-1, keepdims=True)).astype(jnp.bfloat16)
    return jnp.einsum("bhqk,bkhd->bqhd", weights_bf, values, preferred_element_type=jnp.float32).astype(jnp.bfloat16)


def solution(mesh):
    group_size = mesh.shape["tp"]

    def scatter_sum(partial):
        n_batch, seq_len, feat_dim = partial.shape
        split_view = partial.astype(jnp.bfloat16).reshape(n_batch, group_size, seq_len // group_size, feat_dim)
        received = lax.all_to_all(split_view, "tp", 1, 1, tiled=True)
        return jnp.sum(received.astype(jnp.float32), axis=1)

    def device_body(hidden, ln1_gain, ln1_bias, w_qkv, b_qkv, w_out, b_out, ln2_gain, ln2_bias, w_up, b_up, w_down, b_down):
        normed = layer_norm(hidden, ln1_gain, ln1_bias)
        normed_all = lax.all_gather(normed, "tp", axis=1, tiled=True)
        qkv_acc = jnp.einsum("bsd,dthe->bsthe", normed_all, w_qkv, preferred_element_type=jnp.float32)
        qkv_all = (qkv_acc + b_qkv.astype(jnp.float32)).astype(jnp.bfloat16)
        context = causal_attention(qkv_all[:, :, 0], qkv_all[:, :, 1], qkv_all[:, :, 2])
        attn_part = jnp.einsum("bqhd,hde->bqe", context, w_out, preferred_element_type=jnp.float32)
        attn_sum = scatter_sum(attn_part)
        resid_mid = (hidden.astype(jnp.float32) + (attn_sum + b_out.astype(jnp.float32))).astype(jnp.bfloat16)
        normed_mid = layer_norm(resid_mid, ln2_gain, ln2_bias)
        mid_all = lax.all_gather(normed_mid, "tp", axis=1, tiled=True)
        up_proj = jnp.einsum("bsd,df->bsf", mid_all, w_up, preferred_element_type=jnp.float32) + b_up.astype(jnp.float32)
        gelu_out = jax.nn.gelu(up_proj, approximate=True).astype(jnp.bfloat16)
        down_part = jnp.einsum("bsf,fd->bsd", gelu_out, w_down, preferred_element_type=jnp.float32)
        down_sum = scatter_sum(down_part)
        return (resid_mid.astype(jnp.float32) + (down_sum + b_down.astype(jnp.float32))).astype(jnp.bfloat16)

    in_layout = (P("dp", "tp", None), P(), P(), P(None, None, "tp", None), P(None, "tp", None), P("tp", None, None), P(), P(), P(), P(None, "tp"), P("tp"), P("tp", None), P())
    layer_fn = jax.shard_map(device_body, mesh=mesh, in_specs=in_layout, out_specs=P("dp", "tp", None), check_vma=False)
    return layer_fn
```

profile of v0, /device:TPU:0, one launch (start us, length us, event | category | flops | bytes accessed | tf_op | source)
XLA Modules:
  0.0 151.5 jit_solution(13784037075620122108)
XLA Ops:
  6.5 0.0 all-gather.3.cloned.1.call-start
  6.5 1.1 convert_reduce_fusion.3
  7.7 1.2 fusion.56
  8.9 2.0 %fusion.59 = bf16[3,16,4096]{2,1,0:T(8,128)(2,1)} fusion(bf16[3,16,4096]{2,1,0:T(8,128)(2,1)} %param.13, f32[4096]{0:T(1024)} %param.15, f32[4096]{0:T(1024)} %param.14, f32[3,16]{1,0:T(4,128)S(1)} %add_rsqrt_fusion.1, f32[3,16]{1,0:T(4,128)S(1)} %broadcast_multiply_fusion.1), kind=kLoop, calls=%fused_computation.55 | loop fusion | flops 1179648 | bytes 819584 | tf_op jit(solution)/shard_map/convert_element_type | solution.py:14
  10.9 0.0 all-gather.3.cloned.1.call-update
  11.0 0.7 convert_element_type.61
  11.7 18.9 %all-gather.3.cloned.1.call-done = bf16[3,64,4096]{2,1,0:T(8,128)(2,1)} async-done(((bf16[3,16,4096]{2,1,0:T(8,128)(2,1)}), bf16[3,64,4096]{2,1,0:T(8,128)(2,1)}) %all-gather.3.cloned.1.call-update) | async-done | bytes 1572880 | tf_op jit(solution)/shard_map/all_gather | solution.py:40
  30.6 13.7 %add_convert_fusion = bf16[3,64,3,8,128]{4,1,3,2,0:T(8,128)(2,1)S(1)} fusion(bf16[4096,3,8,128]{3,2,1,0:T(8,128)(2,1)} %param.16, bf16[3,64,4096]{2,1,0:T(8,128)(2,1)} %all-gather.3.cloned.1.call-done, f32[3,8,128]{2,1,0:T(8,128)S(1)} %convert_element_type.61), kind=kOutput, calls=%fused_computation.25 | convolution fusion | flops 4833017856 | bytes 27930624 | tf_op jit(solution)/shard_map/bsd,dthe->bsthe/dot_general | solution.py:41
  44.3 0.3 fusion.46
  44.6 0.8 fusion.71
  45.4 5.5 %fusion.16 = bf16[3,64,4096]{2,1,0:T(8,128)(2,1)S(1)} fusion(bf16[8,128,4096]{2,1,0:T(8,128)(2,1)} %param.18, bf16[3,64,3,8,128]{4,1,3,2,0:T(8,128)(2,1)S(1)} %add_convert_fusion, f32[3,8,64]{2,1,0:T(8,128)} %fusion.71, f32[3,8,64,64]{2,3,1,0:T(8,128)S(1)} %fusion.46), kind=kOutput, calls=%fused_computation.12 | convolution fusion | flops 1637058048 | bytes 11540480 | tf_op jit(solution)/shard_map/bqhd,hde->bqe/dot_general | solution.py:44
  50.9 0.0 copy-start.3
  50.9 1.3 copy.16
  52.2 0.0 copy-start
  52.2 0.0 copy-start.1
  52.2 0.0 copy-start.2
  52.2 3.7 %all-to-all-start = ((bf16[3,4,16,4096]{3,2,0,1:T(8,128)(2,1)}), bf16[3,4,16,4096]{3,2,0,1:T(8,128)(2,1)S(1)}, u32[]{:S(2)}, u32[]{:S(2)}) async-start(bf16[3,4,16,4096]{3,2,0,1:T(8,128)(2,1)} %copy.16), calls=%async_computation | async-start | bytes 3145728 | tf_op jit(solution)/shard_map/all_to_all | solution.py:35
  55.9 0.0 copy-start.4
  55.9 0.0 all-gather.5.cloned.1.call-start
  55.9 0.0 copy-done.3
  56.0 19.7 %all-to-all-done = bf16[3,4,16,4096]{3,2,0,1:T(8,128)(2,1)S(1)} async-done(((bf16[3,4,16,4096]{3,2,0,1:T(8,128)(2,1)}), bf16[3,4,16,4096]{3,2,0,1:T(8,128)(2,1)S(1)}, u32[]{:S(2)}, u32[]{:S(2)}) %all-to-all-start) | async-done | bytes 1572896 | tf_op jit(solution)/shard_map/all_to_all | solution.py:35
  75.7 0.2 convert_reduce_fusion.1
  75.9 0.0 copy-done
  75.9 0.2 convert_reduce_fusion.2
  76.2 0.2 fusion.52
  76.4 0.0 copy-done.1
  76.4 0.0 copy-done.2
  76.5 1.0 fusion.55
  77.4 0.0 all-gather.5.cloned.1.call-update
  77.4 0.0 copy-done.4
  77.5 16.8 %all-gather.5.cloned.1.call-done = bf16[3,64,4096]{2,1,0:T(8,128)(2,1)} async-done(((bf16[3,16,4096]{2,1,0:T(8,128)(2,1)}), bf16[3,64,4096]{2,1,0:T(8,128)(2,1)}) %all-gather.5.cloned.1.call-update) | async-done | bytes 1572880 | tf_op jit(solution)/shard_map/all_gather | solution.py:48
  94.2 24.7 %fusion.19 = bf16[3,64,4096]{2,1,0:T(8,128)(2,1)S(1)} fusion(bf16[4096,4096]{1,0:T(8,128)(2,1)} %param.24, bf16[3,64,4096]{2,1,0:T(8,128)(2,1)} %all-gather.5.cloned.1.call-done, bf16[4096,4096]{1,0:T(8,128)(2,1)} %param.22, f32[4096]{0:T(1024)S(1)} %convert_element_type.72), kind=kOutput, calls=%fused_computation.13 | convolution fusion | flops 12893552640 | bytes 70270976 | tf_op jit(solution)/shard_map/bsf,fd->bsd/dot_general | solution.py:51
  118.9 0.0 copy-start.5
  119.0 1.3 copy.17
  120.2 3.6 %all-to-all-start.1 = ((bf16[3,4,16,4096]{3,2,0,1:T(8,128)(2,1)}), bf16[3,4,16,4096]{3,2,0,1:T(8,128)(2,1)S(1)}, u32[]{:S(2)}, u32[]{:S(2)}) async-start(bf16[3,4,16,4096]{3,2,0,1:T(8,128)(2,1)} %copy.17), calls=%async_computation.1 | async-start | bytes 3145728 | tf_op jit(solution)/shard_map/all_to_all | solution.py:35
  123.8 0.0 copy-done.5
  123.8 19.8 %all-to-all-done.1 = bf16[3,4,16,4096]{3,2,0,1:T(8,128)(2,1)S(1)} async-done(((bf16[3,4,16,4096]{3,2,0,1:T(8,128)(2,1)}), bf16[3,4,16,4096]{3,2,0,1:T(8,128)(2,1)S(1)}, u32[]{:S(2)}, u32[]{:S(2)}) %all-to-all-start.1) | async-done | bytes 1572896 | tf_op jit(solution)/shard_map/all_to_all | solution.py:35
  143.6 0.2 convert_reduce_fusion
  143.8 0.9 fusion.61
  (8 shorter events, 0.1 us)
Async XLA Ops:
  6.5 24.0 %all-gather.3.cloned.1.call-start = ((), (), s32[]{:S(2)}) async-start(), calls=%async_computation.2 | async-start | bytes 1966080 | tf_op jit(solution)/shard_map/all_gather | solution.py:40
  50.9 5.0 %copy-start.3 = (bf16[4096]{0:T(1024)(128)(2,1)S(1)}, bf16[4096]{0:T(1024)(128)(2,1)}, u32[]{:S(2)}) copy-start(bf16[4096]{0:T(1024)(128)(2,1)} %param.19) | copy-start | bytes 24580
  52.2 23.8 %copy-start = (bf16[3,16,4096]{2,1,0:T(8,128)(2,1)S(1)}, bf16[3,16,4096]{2,1,0:T(8,128)(2,1)}, u32[]{:S(2)}) copy-start(bf16[3,16,4096]{2,1,0:T(8,128)(2,1)} %param.13) | copy-start | bytes 1179652
  52.2 24.3 %copy-start.1 = (f32[4096]{0:T(1024)S(1)}, f32[4096]{0:T(1024)}, u32[]{:S(2)}) copy-start(f32[4096]{0:T(1024)} %param.21) | copy-start | bytes 49156
  52.2 24.3 %copy-start.2 = (f32[4096]{0:T(1024)S(1)}, f32[4096]{0:T(1024)}, u32[]{:S(2)}) copy-start(f32[4096]{0:T(1024)} %param.20) | copy-start | bytes 49156
  52.2 23.5 %all-to-all-start = ((bf16[3,4,16,4096]{3,2,0,1:T(8,128)(2,1)}), bf16[3,4,16,4096]{3,2,0,1:T(8,128)(2,1)S(1)}, u32[]{:S(2)}, u32[]{:S(2)}) async-start(bf16[3,4,16,4096]{3,2,0,1:T(8,128)(2,1)} %copy.16), calls=%async_computation | async-start | bytes 3145728 | tf_op jit(solution)/shard_map/all_to_all | solution.py:35
  55.9 21.6 %copy-start.4 = (bf16[4096]{0:T(1024)(128)(2,1)S(1)}, bf16[4096]{0:T(1024)(128)(2,1)}, u32[]{:S(2)}) copy-start(bf16[4096]{0:T(1024)(128)(2,1)} %param.23) | copy-start | bytes 24580
  55.9 38.3 %all-gather.5.cloned.1.call-start = ((), (), s32[]{:S(2)}) async-start(), calls=%async_computation.3 | async-start | bytes 1966080 | tf_op jit(solution)/shard_map/all_gather | solution.py:48
  118.9 4.8 %copy-start.5 = (bf16[4096]{0:T(1024)(128)(2,1)S(1)}, bf16[4096]{0:T(1024)(128)(2,1)}, u32[]{:S(2)}) copy-start(bf16[4096]{0:T(1024)(128)(2,1)} %param.25) | copy-start | bytes 24580
  120.2 23.4 %all-to-all-start.1 = ((bf16[3,4,16,4096]{3,2,0,1:T(8,128)(2,1)}), bf16[3,4,16,4096]{3,2,0,1:T(8,128)(2,1)S(1)}, u32[]{:S(2)}, u32[]{:S(2)}) async-start(bf16[3,4,16,4096]{3,2,0,1:T(8,128)(2,1)} %copy.17), calls=%async_computation.1 | async-start | bytes 3145728 | tf_op jit(solution)/shard_map/all_to_all | solution.py:35
Sparse Core Ops, SparseCore 0:
  11.1 19.4 all-gather.2
  77.6 16.6 all-gather.4
where the time goes:
time: 152 us
  waiting for transfers between devices  75.2 us (49%)
  matrix products  44.2 us (29%)
  between operations  13.6 us (9%)
  other arithmetic  8.65 us (6%)
  starting transfers between devices  7.3 us (5%)
  local copies, waits for them, and re-layouts  2.57 us (2%)
    all_to_all x2, waiting for transfers between devices, scatter_sum(): received = lax.all_to_all(split_view, 'tp', 1, 1, tiled=True)  39.5 us
    dot_general x1, matrix products, device_body(): jnp.einsum('bsf,fd->bsd', gelu_out, w_down, preferred_element_type=jnp.fl...  24.7 us
    all_gather x1, waiting for transfers between devices, device_body(): normed_all = lax.all_gather(normed, 'tp', axis=1, tiled=True)  18.9 us
    all_gather x1, waiting for transfers between devices, device_body(): mid_all = lax.all_gather(normed_mid, 'tp', axis=1, tiled=True)  16.8 us
    dot_general x1, matrix products, device_body(): jnp.einsum('bsd,dthe->bsthe', normed_all, w_qkv, preferred_element_type=j...  13.7 us
    all_to_all x2, starting transfers between devices, scatter_sum(): received = lax.all_to_all(split_view, 'tp', 1, 1, tiled=True)  7.25 us
    dot_general x1, matrix products, device_body(): jnp.einsum('bqhd,hde->bqe', context, w_out, preferred_element_type=jnp.fl...  5.49 us
  transfers between devices with their start and end apart: 4, of which 4 were waited for; matrix products, arithmetic and copies ran while one was open for 0% of the time, Pallas kernels for 0%

commit v1 on v0

v1 whole, which is shorter than its diff:
```python
import jax
import jax.numpy as jnp
from jax import lax
from jax.experimental import pallas as pl
from jax.experimental.pallas import tpu as pltpu
from jax.sharding import PartitionSpec as P

MESH = pl.DeviceIdType.MESH
F32, BF16 = jnp.float32, jnp.bfloat16

LN_EPS = 1e-5
N_BATCH, BLOCK, D = 3, 16, 4096
ROWS = N_BATCH * BLOCK
TOKENS = 4 * ROWS
HEADS, HEAD_DIM = 8, 128
FF = 4096
QKV = 3 * HEADS * HEAD_DIM

PK, PN = 1024, 512
KC = D // PK
NC = D // PN
N_QKV, N_OUT, N_UP, N_DOWN = 24, 8, 32, 32
G_OUT, G_UP, G_DOWN = 24, 32, 64
SLOTS = 36
STAGE_ROWS, STAGES = 256, 4
STEPS = D // STAGE_ROWS


def kernel(x_hbm, g1_hbm, b1_hbm, wqkv_hbm, bqkv_hbm, wout_hbm, bout_hbm, g2_hbm, b2_hbm, wup_hbm, bup_hbm, wdown_hbm, bdown_hbm, out_hbm,
           stage, slots, x_own, h_all, x1_all, acc, qkv_bf, ctx, u, own, pf,
           psend1, prec1, xsend1, xrec1, psend2, prec2, xsend2, xrec2, xsum, stats, ostage,
           vec_f32, vec_bf, bqkv_v, rows, bqkv_row,
           stage_sem, slot_sem, small_sem, x_sem, out_sem,
           ag_s, ag_r, ag2_s, ag2_r, st_s, st_r, rs1_s, rs1_r, rs2_s, rs2_r):
    dp = lax.axis_index("dp")
    me = lax.axis_index("tp")
    core = lax.rem(me, 2)
    chip = lax.div(me, 2)
    partner = me + 1 - 2 * core
    cross = lax.rem(me + 2, 4)
    far = lax.rem(partner + 2, 4)
    other_core = 1 - core
    other_chip = 1 - chip

    def stage_copy(i):
        return pltpu.make_async_copy(wqkv_hbm.at[pl.ds(i * STAGE_ROWS, STAGE_ROWS)], stage.at[lax.rem(i, STAGES)], stage_sem.at[lax.rem(i, STAGES)])

    def to_slot(src, g):
        s = lax.rem(g, SLOTS)
        return pltpu.make_async_copy(src, slots.at[s], slot_sem.at[s])

    def out_copy(n):
        return to_slot(wout_hbm.at[:, pl.ds(n * PN, PN)], G_OUT + n)

    def up_copy(i):
        k, n = lax.div(i, NC), lax.rem(i, NC)
        return to_slot(wup_hbm.at[pl.ds(pl.multiple_of(k * PK, PK), PK), pl.ds(pl.multiple_of(n * PN, PN), PN)], G_UP + i)

    def down_copy(i):
        n, k = lax.div(i, KC), lax.rem(i, KC)
        return to_slot(wdown_hbm.at[pl.ds(pl.multiple_of(k * PK, PK), PK), pl.ds(pl.multiple_of(n * PN, PN), PN)], G_DOWN + i)

    x_copy = pltpu.make_async_copy(x_hbm, x_own, x_sem.at[0])
    x_copy.start()
    smalls = [pltpu.make_async_copy(src, vec_f32.at[i], small_sem.at[i]) for i, src in enumerate((g1_hbm, b1_hbm, g2_hbm, b2_hbm))]
    smalls += [pltpu.make_async_copy(src, vec_bf.at[i], small_sem.at[4 + i]) for i, src in enumerate((bout_hbm, bup_hbm, bdown_hbm))]
    smalls += [pltpu.make_async_copy(bqkv_hbm, bqkv_v, small_sem.at[7])]
    for c in smalls:
        c.start()
    for i in range(STAGES):
        stage_copy(i).start()

    barrier = pltpu.get_barrier_semaphore()
    for peer in (partner, cross):
        pl.semaphore_signal(barrier, inc=1, device_id=(dp, peer), device_id_type=MESH)

    for c in smalls:
        c.wait()
    for i in range(4):
        for j in range(32):
            rows[i, :, j * 128:(j + 1) * 128] = vec_f32[i, j:j + 1, :]
    for i in range(3):
        vals = vec_bf[i].astype(F32)
        for j in range(32):
            rows[4 + i, :, j * 128:(j + 1) * 128] = vals[j:j + 1, :]
    for t in range(3):
        vals = bqkv_v[t].astype(F32)
        for j in range(HEADS):
            bqkv_row[:, (t * HEADS + j) * 128:(t * HEADS + j + 1) * 128] = vals[j:j + 1, :]
    G1, B1, G2, B2, BOUT, BUP, BDOWN = range(7)

    def row_stats(x):
        mean = jnp.mean(x, axis=-1, keepdims=True)
        centered = x - mean
        var = jnp.mean(centered * centered, axis=-1, keepdims=True)
        return mean, lax.rsqrt(var + LN_EPS)

    x_copy.wait()
    for b in range(N_BATCH):
        r = pl.ds(b * BLOCK, BLOCK)
        xf = x_own[r, :].astype(F32)
        mean, rstd = row_stats(xf)
        h_all[me, r, :] = ((xf - mean) * rstd * rows[G1] + rows[B1]).astype(BF16)

    pl.semaphore_wait(barrier, 2)

    def push(buf, block, c, width, s, r, which, peer):
        ref = buf.at[block, :, pl.ds(c * width, width)]
        return pltpu.make_async_remote_copy(src_ref=ref, dst_ref=ref, send_sem=s.at[which, c], recv_sem=r.at[which, c], device_id=(dp, peer), device_id_type=MESH)

    def ag1(which, block, peer, c):
        return push(h_all, block, c, PK, ag_s, ag_r, which, peer)

    for c in range(KC):
        ag1(0, me, cross, c).start()
    for c in range(KC):
        ag1(1, me, partner, c).start()

    def ag1_forward(c):
        ag1(0, cross, cross, c).wait_recv()
        ag1(2, cross, partner, c).start()

    def relayout(i, carry):
        stage_copy(i).wait()
        s = lax.rem(i, STAGES)
        k, off = lax.div(i, 4), lax.rem(i, 4)
        r = pl.ds(pl.multiple_of(off * STAGE_ROWS, STAGE_ROWS), STAGE_ROWS)
        for t in range(3):
            w = stage[s, :, t].reshape(STAGE_ROWS, HEADS * HEAD_DIM)
            slots[k * 6 + 2 * t, r, :] = w[:, :PN]
            slots[k * 6 + 2 * t + 1, r, :] = w[:, PN:]

        @pl.when(i + STAGES < STEPS)
        def _():
            stage_copy(i + STAGES).start()

        return carry

    lax.fori_loop(0, STEPS - STAGES, relayout, 0)
    for n in range(N_OUT):
        out_copy(n).start()
    for i in range(SLOTS - G_UP):
        up_copy(i).start()
    lax.fori_loop(STEPS - STAGES, STEPS, relayout, 0)

    def tokens(buf, c):
        return buf[:, :, c * PK:(c + 1) * PK].reshape(TOKENS, PK)

    def qkv_chunk(c):
        ag1(1, partner, partner, c).wait_recv()
        ag1(2, far, partner, c).wait_recv()
        h = tokens(h_all, c)

        def group(q, carry):
            for m in range(3):
                n = q * 3 + m
                cols = pl.ds(pl.multiple_of(n * PN, PN), PN)
                part = jnp.dot(h, slots[c * 6 + n], preferred_element_type=F32)
                if c:
                    part = part + acc[:, cols]
                if c < KC - 1:
                    acc[:, cols] = part
                else:
                    val = (part + bqkv_row[:, cols]).astype(BF16)
                    for d in range(4):
                        for b in range(N_BATCH):
                            qkv_bf[b, d * BLOCK:(d + 1) * BLOCK, cols] = val[d * ROWS + b * BLOCK:d * ROWS + (b + 1) * BLOCK]
            for m in range(3):
                up_copy(c * 6 + q * 3 + m + SLOTS - G_UP).start()
            return carry

        lax.fori_loop(0, 2, group, 0)

    ag1_forward(0)
    ag1_forward(1)
    qkv_chunk(0)
    ag1_forward(2)
    qkv_chunk(1)
    ag1_forward(3)
    qkv_chunk(2)
    qkv_chunk(3)
    for c in range(KC):
        ag1(0, me, cross, c).wait_send()
        ag1(1, me, partner, c).wait_send()
        ag1(2, cross, partner, c).wait_send()

    def attend(b, carry):
        seq = N_BATCH * 0 + 4 * BLOCK
        causal = lax.broadcasted_iota(jnp.int32, (seq, seq), 0) >= lax.broadcasted_iota(jnp.int32, (seq, seq), 1)
        r = pl.ds(pl.multiple_of(b * BLOCK, BLOCK), BLOCK)
        for j in range(HEADS):
            q, k, v = (qkv_bf[b, :, (t * HEADS + j) * HEAD_DIM:(t * HEADS + j + 1) * HEAD_DIM] for t in range(3))
            logits = lax.dot_general(q, k, (((1,), (1,)), ((), ())), preferred_element_type=F32) * HEAD_DIM ** -0.5
            logits = jnp.where(causal, logits, -1e30)
            e = jnp.exp(logits - jnp.max(logits, axis=-1, keepdims=True))
            p = (e * (1.0 / jnp.sum(e, axis=-1, keepdims=True))).astype(BF16)
            o = jnp.dot(p, v, preferred_element_type=F32).astype(BF16)
            for d in range(4):
                ctx[d, r, j * HEAD_DIM:(j + 1) * HEAD_DIM] = o[d * BLOCK:(d + 1) * BLOCK]
        return carry

    lax.fori_loop(0, N_BATCH, attend, 0)

    def rs_pair(psend, prec, s, r, n):
        return pltpu.make_async_remote_copy(src_ref=psend.at[n], dst_ref=prec.at[n], send_sem=s.at[0, n], recv_sem=r.at[0, n], device_id=(dp, partner), device_id_type=MESH)

    def rs_cross(xsend, xrec, s, r, n):
        return pltpu.make_async_remote_copy(src_ref=xsend.at[n], dst_ref=xrec.at[n], send_sem=s.at[1, n], recv_sem=r.at[1, n], device_id=(dp, cross), device_id_type=MESH)

    def rs_a(part, psend, prec, s, r, n):
        pf[...] = part.reshape(4, ROWS, PN)
        for q in range(2):
            psend[n, q] = pf[2 * q + other_core].astype(BF16)
            own[n, q] = pf[2 * q + core]
        rs_pair(psend, prec, s, r, n).start()

    def rs_b(psend, prec, xsend, xrec, s, r, n):
        rs_pair(psend, prec, s, r, n).wait_recv()
        xsend[n] = (own[n, other_chip] + prec[n, other_chip].astype(F32)).astype(BF16)
        rs_cross(xsend, xrec, s, r, n).start()
        xsum[n] = own[n, chip] + prec[n, chip].astype(F32)

    def rs_c(xsend, xrec, s, r, n):
        rs_cross(xsend, xrec, s, r, n).wait_recv()
        return xsum[n] + xrec[n].astype(F32)

    ctx_rows = ctx[...].reshape(TOKENS, HEADS * HEAD_DIM)

    def out_a(n):
        out_copy(n).wait()
        rs_a(jnp.dot(ctx_rows, slots[(G_OUT + n) % SLOTS], preferred_element_type=F32), psend1, prec1, rs1_s, rs1_r, n)
        g = G_OUT + n + SLOTS
        (up_copy(g - G_UP) if g < G_DOWN else down_copy(g - G_DOWN)).start()

    def out_b(n):
        rs_b(psend1, prec1, xsend1, xrec1, rs1_s, rs1_r, n)

    def ag2(which, block, peer, c):
        return push(x1_all, block, c, PK, ag2_s, ag2_r, which, peer)

    def st(which, block, peer):
        ref = stats.at[block]
        return pltpu.make_async_remote_copy(src_ref=ref, dst_ref=ref, send_sem=st_s.at[which], recv_sem=st_r.at[which], device_id=(dp, peer), device_id_type=MESH)

    lead = 4
    for n in range(NC):
        out_a(n)
        if n >= lead:
            out_b(n - lead)
    for n in range(NC - lead, NC):
        out_b(n)
    for n in range(NC):
        cols = slice(n * PN, (n + 1) * PN)
        total = rs_c(xsend1, xrec1, rs1_s, rs1_r, n)
        x1_all[me, :, cols] = (x_own[:, cols].astype(F32) + (total + rows[BOUT, :, cols])).astype(BF16)
        if n == 1:
            ag2(0, me, cross, 0).start()
            ag2(1, me, partner, 0).start()
    for b in range(N_BATCH):
        r = pl.ds(b * BLOCK, BLOCK)
        mean, rstd = row_stats(x1_all[me, r, :].astype(F32))
        lane = lax.broadcasted_iota(jnp.int32, (BLOCK, 128), 1)
        stats[me, r, :] = jnp.where(lane == 0, mean, rstd)
    st(0, me, cross).start()
    st(1, me, partner).start()
    for c in range(1, KC):
        ag2(0, me, cross, c).start()
        ag2(1, me, partner, c).start()
    st(0, cross, cross).wait_recv()
    st(2, cross, partner).start()

    def ag2_forward(c):
        ag2(0, cross, cross, c).wait_recv()
        ag2(2, cross, partner, c).start()

    def up_chunk(c):
        ag2(1, partner, partner, c).wait_recv()
        ag2(2, far, partner, c).wait_recv()
        cols = slice(c * PK, (c + 1) * PK)
        for d in range(4):
            xf = x1_all[d, :, cols].astype(F32)
            h_all[d, :, cols] = ((xf - stats[d, :, 0:1]) * stats[d, :, 1:2] * rows[G2, :, cols] + rows[B2, :, cols]).astype(BF16)
        h = tokens(h_all, c)

        def group(q, carry):
            for m in range(4):
                up_copy(c * NC + q * 4 + m).wait()
            for m in range(4):
                n = q * 4 + m
                wide = pl.ds(pl.multiple_of(n * PN, PN), PN)
                part = jnp.dot(h, slots[lax.rem(G_UP + c * NC + n, SLOTS)], preferred_element_type=F32)
                if c:
                    part = part + acc[:, wide]
                if c < KC - 1:
                    acc[:, wide] = part
                else:
                    u[:, wide] = jax.nn.gelu(part + rows[BUP, :, wide], approximate=True).astype(BF16)
            for m in range(4):
                i = c * NC + q * 4 + m + G_UP + SLOTS - G_DOWN

                @pl.when(i < N_DOWN)
                def _():
                    down_copy(i).start()

            return carry

        lax.fori_loop(0, 2, group, 0)

    ag2_forward(0)
    st(1, partner, partner).wait_recv()
    st(2, far, partner).wait_recv()
    ag2_forward(1)
    up_chunk(0)
    ag2_forward(2)
    up_chunk(1)
    ag2_forward(3)
    up_chunk(2)
    up_chunk(3)

    def down_a(n):
        for k in range(KC):
            down_copy(n * KC + k).wait()
        part = None
        for k in range(KC):
            term = jnp.dot(u[:, k * PK:(k + 1) * PK], slots[(G_DOWN + n * KC + k) % SLOTS], preferred_element_type=F32)
            part = term if part is None else part + term
        rs_a(part, psend2, prec2, rs2_s, rs2_r, n)

    def out_write(n):
        cols = pl.ds(n * PN, PN)
        return pltpu.make_async_copy(ostage.at[:, cols], out_hbm.at[:, cols], out_sem.at[n])

    def down_b(n):
        rs_b(psend2, prec2, xsend2, xrec2, rs2_s, rs2_r, n)

    def down_c(n):
        cols = slice(n * PN, (n + 1) * PN)
        total = rs_c(xsend2, xrec2, rs2_s, rs2_r, n)
        ostage[:, cols] = (x1_all[me, :, cols].astype(F32) + (total + rows[BDOWN, :, cols])).astype(BF16)
        out_write(n).start()

    for n in range(NC):
        down_a(n)
        if n >= 1:
            down_b(n - 1)
    down_b(NC - 1)
    for n in range(NC):
        down_c(n)

    for n in range(NC):
        out_write(n).wait()
        rs_pair(psend1, prec1, rs1_s, rs1_r, n).wait_send()
        rs_cross(xsend1, xrec1, rs1_s, rs1_r, n).wait_send()
        rs_pair(psend2, prec2, rs2_s, rs2_r, n).wait_send()
        rs_cross(xsend2, xrec2, rs2_s, rs2_r, n).wait_send()
    for c in range(KC):
        ag2(0, me, cross, c).wait_send()
        ag2(1, me, partner, c).wait_send()
        ag2(2, cross, partner, c).wait_send()
    st(0, me, cross).wait_send()
    st(1, me, partner).wait_send()
    st(2, cross, partner).wait_send()


def solution(mesh):
    def device_body(hidden, ln1_gain, ln1_bias, w_qkv, b_qkv, w_out, b_out, ln2_gain, ln2_bias, w_up, b_up, w_down, b_down):
        args = (hidden.reshape(ROWS, D), ln1_gain.reshape(32, 128), ln1_bias.reshape(32, 128), w_qkv, b_qkv, w_out.reshape(HEADS * HEAD_DIM, D),
                b_out.reshape(32, 128), ln2_gain.reshape(32, 128), ln2_bias.reshape(32, 128), w_up, b_up.reshape(32, 128), w_down, b_down.reshape(32, 128))
        hbm = pl.BlockSpec(memory_space=pltpu.HBM)
        dma = pltpu.SemaphoreType.DMA
        rs_buffers = [pltpu.VMEM((NC, 2, ROWS, PN), BF16), pltpu.VMEM((NC, 2, ROWS, PN), BF16), pltpu.VMEM((NC, ROWS, PN), BF16), pltpu.VMEM((NC, ROWS, PN), BF16)]
        result = pl.pallas_call(
            kernel,
            out_shape=jax.ShapeDtypeStruct((ROWS, D), BF16),
            in_specs=[hbm] * len(args),
            out_specs=hbm,
            scratch_shapes=[
                pltpu.VMEM((STAGES, STAGE_ROWS, 3, HEADS, HEAD_DIM), BF16),
                pltpu.VMEM((SLOTS, PK, PN), BF16),
                pltpu.VMEM((ROWS, D), BF16),
                pltpu.VMEM((4, ROWS, D), BF16),
                pltpu.VMEM((4, ROWS, D), BF16),
                pltpu.VMEM((TOKENS, FF), F32),
                pltpu.VMEM((N_BATCH, 4 * BLOCK, QKV), BF16),
                pltpu.VMEM((4, ROWS, HEADS * HEAD_DIM), BF16),
                pltpu.VMEM((TOKENS, FF), BF16),
                pltpu.VMEM((NC, 2, ROWS, PN), F32),
                pltpu.VMEM((4, ROWS, PN), F32),
                *rs_buffers,
                *rs_buffers,
                pltpu.VMEM((NC, ROWS, PN), F32),
                pltpu.VMEM((4, ROWS, 128), F32),
                pltpu.VMEM((ROWS, D), BF16),
                pltpu.VMEM((4, 32, 128), F32),
                pltpu.VMEM((3, 32, 128), BF16),
                pltpu.VMEM((3, HEADS, HEAD_DIM), BF16),
                pltpu.VMEM((7, 1, D), F32),
                pltpu.VMEM((1, QKV), F32),
                dma((STAGES,)), dma((SLOTS,)), dma((8,)), dma((1,)), dma((NC,)),
                dma((3, KC)), dma((3, KC)), dma((3, KC)), dma((3, KC)), dma((3,)), dma((3,)),
                dma((2, NC)), dma((2, NC)), dma((2, NC)), dma((2, NC)),
            ],
            compiler_params=pltpu.CompilerParams(collective_id=0, has_side_effects=True, vmem_limit_bytes=67_043_328),
            name="decoder_layer",
        )(*args)
        return result.reshape(hidden.shape)

    in_layout = (P("dp", "tp", None), P(), P(), P(None, None, "tp", None), P(None, "tp", None), P("tp", None, None), P(), P(), P(), P(None, "tp"), P("tp"), P("tp", None), P())
    return jax.shard_map(device_body, mesh=mesh, in_specs=in_layout, out_specs=P("dp", "tp", None), check_vma=False)
```

time: 152 us -> 73.1 us (0.48)
  waiting for transfers between devices: 75.2 us -> 0 us
  Pallas kernels: 0 us -> 71.1 us
  matrix products: 44.2 us -> 0 us
  between operations: 13.6 us -> 0.01 us
  other arithmetic: 8.65 us -> 0 us
  starting transfers between devices: 7.3 us -> 0 us
    pallas_call x0 -> x1, Pallas kernels: none -> 71.1 us  [device_body(): pl.pallas_call(kernel, out_shape=jax.ShapeDtypeStruct((ROWS, D), BF16), i...]
    dot_general x4 -> x0, matrix products: 44.2 us -> none  [the longest x1 24.7 us: device_body(): jnp.einsum('bsf,fd->bsd', gelu_out, w_down, preferred_element_type=jnp.fl...]
    all_to_all x2 -> x0, waiting for transfers between devices: 39.5 us -> none  [scatter_sum(): received = lax.all_to_all(split_view, 'tp', 1, 1, tiled=True)]
    all_gather x2 -> x0, waiting for transfers between devices: 35.7 us -> none  [the longest x1 18.9 us: device_body(): normed_all = lax.all_gather(normed, 'tp', axis=1, tiled=True)]
    all_to_all x2 -> x0, starting transfers between devices: 7.25 us -> none  [scatter_sum(): received = lax.all_to_all(split_view, 'tp', 1, 1, tiled=True)]
    convert_element_type x7 -> x0, other arithmetic: 4.51 us -> none  [the longest x2 2.94 us: layer_norm(): (centered * lax.rsqrt(variance + LN_EPS) * gain_vec + shift_vec).astype(j...]
    reduce_sum x6 -> x0, other arithmetic: 3.29 us -> none  [the longest x2 1.48 us: layer_norm(): variance = jnp.mean(centered * centered, axis=-1, keepdims=True)]
    reshape x2 -> x0, local copies, waits for them, and re-layouts: 2.53 us -> none  [scatter_sum(): partial.astype(jnp.bfloat16)]
  transfers between devices with their start and end apart: 4 -> 0, of which waited for: 4 -> 0; matrix products, arithmetic and copies ran while one was open for 0% -> 0% of each run, Pallas kernels for 0% -> 0%
where the time goes in v1:
time: 73.1 us; the launch traced here: 72.9 us
  Pallas kernels  71.1 us (97%)
  local copies, waits for them, and re-layouts  1.77 us (2%)
    pallas_call x1, Pallas kernels, device_body(): pl.pallas_call(kernel, out_shape=jax.ShapeDtypeStruct((ROWS, D), BF16), i...  71.1 us
    unnamed x1, local copies, waits for them, and re-layouts  1.77 us

profile of v1, /device:TPU:0, one launch (start us, length us, event | category | flops | bytes accessed | tf_op | source)
XLA Modules:
  0.0 72.9 jit_solution(4966823440246877328)
XLA Ops:
  0.0 71.1 %decoder_layer.1 = bf16[48,4096]{1,0:T(8,128)(2,1)} custom-call(bf16[48,4096]{1,0:T(8,128)(2,1)} %bitcast.12, f32[32,128]{1,0:T(8,128)} %bitcast.13, f32[32,128]{1,0:T(8,128)} %bitcast.14, bf16[4096,3,8,128]{3,2,1,0:T(8,128)(2,1)} %wqkv_hbm.1, bf16[3,8,128]{2,1,0:T(8,128)(2,1)} %bqkv_hbm.1, bf16[1024,4096]{1,0:T(8,128)(2,1)} %bitcast.10, ...), custom_call_target="tpu_custom_call" | custom-call | tf_op jit(solution)/shard_map/decoder_layer/pallas_call | solution.py:372
  71.1 1.8 %copy.15 = bf16[3,16,4096]{2,1,0:T(8,128)(2,1)} copy(bf16[3,16,4096]{2,1,0:T(8,128)(2,1)} %bitcast.11) | data formatting | bytes 786432

commit v2 on v1

v2 whole, which is shorter than its diff:
```python
import jax
import jax.numpy as jnp
from jax import lax
from jax.experimental import pallas as pl
from jax.experimental.pallas import tpu as pltpu
from jax.sharding import PartitionSpec as P

MESH = pl.DeviceIdType.MESH
F32, BF16 = jnp.float32, jnp.bfloat16

LN_EPS = 1e-5
N_BATCH, BLOCK, D = 3, 16, 4096
ROWS = N_BATCH * BLOCK
TOKENS = 4 * ROWS
HEADS, HEAD_DIM = 8, 128
FF = 4096
QKV = 3 * HEADS * HEAD_DIM

PK, PN = 1024, 512
KC = D // PK
NC = D // PN
N_QKV, N_OUT, N_UP, N_DOWN = 24, 8, 32, 32
G_OUT, G_UP, G_DOWN = 24, 32, 64
SLOTS = 36
STAGE_ROWS, STAGES = 256, 4
STEPS = D // STAGE_ROWS


def kernel(x_hbm, g1_hbm, b1_hbm, wqkv_hbm, bqkv_hbm, wout_hbm, bout_hbm, g2_hbm, b2_hbm, wup_hbm, bup_hbm, wdown_hbm, bdown_hbm, out_ref,
           stage, slots, x_own, h_all, x1_all, acc, qkv_bf, ctx, u, own, pf,
           psend1, prec1, xsend1, xrec1, psend2, prec2, xsend2, xrec2, xsum, stats, stat_cols, square,
           vec_f32, vec_bf, bqkv_v, rows, bqkv_row, mask,
           stage_sem, slot_sem, small_sem, x_sem,
           ag_s, ag_r, ag2_s, ag2_r, st_s, st_r, rs1_s, rs1_r, rs2_s, rs2_r):
    dp = lax.axis_index("dp")
    me = lax.axis_index("tp")
    core = lax.rem(me, 2)
    chip = lax.div(me, 2)
    partner = me + 1 - 2 * core
    cross = lax.rem(me + 2, 4)
    far = lax.rem(partner + 2, 4)
    other_core = 1 - core
    other_chip = 1 - chip

    def stage_copy(i):
        return pltpu.make_async_copy(wqkv_hbm.at[pl.ds(i * STAGE_ROWS, STAGE_ROWS)], stage.at[lax.rem(i, STAGES)], stage_sem.at[lax.rem(i, STAGES)])

    def to_slot(src, g):
        s = lax.rem(g, SLOTS)
        return pltpu.make_async_copy(src, slots.at[s], slot_sem.at[s])

    def out_copy(n):
        return to_slot(wout_hbm.at[:, pl.ds(n * PN, PN)], G_OUT + n)

    def up_copy(i):
        k, n = lax.div(i, NC), lax.rem(i, NC)
        return to_slot(wup_hbm.at[pl.ds(pl.multiple_of(k * PK, PK), PK), pl.ds(pl.multiple_of(n * PN, PN), PN)], G_UP + i)

    def down_copy(i):
        n, k = lax.div(i, KC), lax.rem(i, KC)
        return to_slot(wdown_hbm.at[pl.ds(pl.multiple_of(k * PK, PK), PK), pl.ds(pl.multiple_of(n * PN, PN), PN)], G_DOWN + i)

    barrier = pltpu.get_barrier_semaphore()
    for peer in (partner, cross, far):
        pl.semaphore_signal(barrier, inc=1, device_id=(dp, peer), device_id_type=MESH)
    G1, B1, G2, B2, BOUT, BUP, BDOWN = range(7)
    x_copy = pltpu.make_async_copy(x_hbm, x_own, x_sem.at[0])
    smalls = [pltpu.make_async_copy(src, vec_f32.at[i], small_sem.at[i]) for i, src in enumerate((g1_hbm, b1_hbm, g2_hbm, b2_hbm))]
    smalls += [pltpu.make_async_copy(src, vec_bf.at[i], small_sem.at[4 + i]) for i, src in enumerate((bout_hbm, bup_hbm, bdown_hbm))]
    smalls += [pltpu.make_async_copy(bqkv_hbm, bqkv_v, small_sem.at[7])]
    smalls[G1].start()
    smalls[B1].start()
    x_copy.start()

    def f32_row(i):
        for j in range(32):
            rows[i, :, j * 128:(j + 1) * 128] = vec_f32[i, j:j + 1, :]

    def row_stats(x):
        mean = jnp.mean(x, axis=-1, keepdims=True)
        centered = x - mean
        var = jnp.mean(centered * centered, axis=-1, keepdims=True)
        return mean, lax.rsqrt(var + LN_EPS)

    for i in (G1, B1):
        smalls[i].wait()
        f32_row(i)
    x_copy.wait()
    for i in range(STAGES):
        stage_copy(i).start()
    for c in smalls[2:]:
        c.start()
    for b in range(N_BATCH):
        r = pl.ds(b * BLOCK, BLOCK)
        xf = x_own[r, :].astype(F32)
        mean, rstd = row_stats(xf)
        h_all[me, r, :] = ((xf - mean) * rstd * rows[G1] + rows[B1]).astype(BF16)

    pl.semaphore_wait(barrier, 3)

    def push(buf, block, c, width, s, r, which, peer):
        ref = buf.at[block, :, pl.ds(c * width, width)]
        return pltpu.make_async_remote_copy(src_ref=ref, dst_ref=ref, send_sem=s.at[which, c], recv_sem=r.at[which, c], device_id=(dp, peer), device_id_type=MESH)

    def ag1(which, block, peer, c):
        return push(h_all, block, c, PK, ag_s, ag_r, which, peer)

    for c in range(KC):
        ag1(0, me, cross, c).start()
    for c in range(KC):
        ag1(1, me, partner, c).start()

    for c in smalls[2:]:
        c.wait()
    for i in (G2, B2):
        f32_row(i)
    for i in range(3):
        vals = vec_bf[i].astype(F32)
        for j in range(32):
            rows[4 + i, :, j * 128:(j + 1) * 128] = vals[j:j + 1, :]
    for t in range(3):
        vals = bqkv_v[t].astype(F32)
        for j in range(HEADS):
            bqkv_row[:, (t * HEADS + j) * 128:(t * HEADS + j + 1) * 128] = vals[j:j + 1, :]

    def token_place(axis):
        t = lax.broadcasted_iota(jnp.int32, (TOKENS, TOKENS), axis)
        d = sum((t >= ROWS * i).astype(jnp.int32) for i in range(1, 4))
        t = t - ROWS * d
        b = sum((t >= BLOCK * i).astype(jnp.int32) for i in range(1, N_BATCH))
        return b, d * BLOCK + t - BLOCK * b

    (q_seq, q_pos), (k_seq, k_pos) = token_place(0), token_place(1)
    square[...] = jnp.zeros_like(square)
    mask[...] = ((q_seq == k_seq) & (q_pos >= k_pos)).astype(F32)

    def ag1_forward(c):
        ag1(0, cross, cross, c).wait_recv()
        ag1(2, cross, partner, c).start()

    def relayout(i):
        s = lax.rem(i, STAGES)
        k, off = lax.div(i, 4), lax.rem(i, 4)
        r = pl.ds(pl.multiple_of(off * STAGE_ROWS, STAGE_ROWS), STAGE_ROWS)
        for t in range(3):
            w = stage[s, :, t].reshape(STAGE_ROWS, HEADS * HEAD_DIM)
            slots[k * 6 + 2 * t, r, :] = w[:, :PN]
            slots[k * 6 + 2 * t + 1, r, :] = w[:, PN:]

    def relayout_step(i, carry):
        stage_copy(i).wait()
        relayout(i)

        @pl.when(i + STAGES < STEPS)
        def _():
            stage_copy(i + STAGES).start()

        return carry

    lax.fori_loop(0, STEPS - STAGES, relayout_step, 0)
    for n in range(N_OUT):
        out_copy(n).start()
    for i in range(SLOTS - G_UP):
        up_copy(i).start()
    lax.fori_loop(STEPS - STAGES, STEPS, relayout_step, 0)

    def tokens(buf, c):
        return buf[:, :, c * PK:(c + 1) * PK].reshape(TOKENS, PK)

    def qkv_chunk(c):
        ag1(1, partner, partner, c).wait_recv()
        ag1(2, far, partner, c).wait_recv()
        h = tokens(h_all, c)
        for n in range(6):
            cols = slice(n * PN, (n + 1) * PN)
            part = jnp.dot(h, slots[c * 6 + n], preferred_element_type=F32)
            if c:
                part = part + acc[:, cols]
            if c < KC - 1:
                acc[:, cols] = part
            else:
                qkv_bf[:, cols] = (part + bqkv_row[:, cols]).astype(BF16)
        for n in range(6):
            up_copy(c * 6 + n + SLOTS - G_UP).start()

    ag1_forward(0)
    for c in range(KC):
        if c < KC - 1:
            ag1_forward(c + 1)
        qkv_chunk(c)
    for c in range(KC):
        ag1(0, me, cross, c).wait_send()
        ag1(1, me, partner, c).wait_send()
        ag1(2, cross, partner, c).wait_send()

    keep = mask[...] > 0.5
    for first in range(0, HEADS, 4):
        heads = range(first, first + 4)

        def part_of(t, j):
            return qkv_bf[:, (t * HEADS + j) * HEAD_DIM:(t * HEADS + j + 1) * HEAD_DIM]

        logits = [lax.dot_general(part_of(0, j), part_of(1, j), (((1,), (1,)), ((), ())), preferred_element_type=F32) for j in heads]
        logits = [jnp.where(keep, x * HEAD_DIM ** -0.5, -1e30) for x in logits]
        tops = [jnp.max(x, axis=-1, keepdims=True) for x in logits]
        es = [jnp.exp(x - t) for x, t in zip(logits, tops)]
        sums = [jnp.sum(e, axis=-1, keepdims=True) for e in es]
        ps = [(e * (1.0 / z)).astype(BF16) for e, z in zip(es, sums)]
        for j, p in zip(heads, ps):
            ctx[:, j * HEAD_DIM:(j + 1) * HEAD_DIM] = jnp.dot(p, part_of(2, j), preferred_element_type=F32).astype(BF16)

    def rs_pair(psend, prec, s, r, n):
        return pltpu.make_async_remote_copy(src_ref=psend.at[n], dst_ref=prec.at[n], send_sem=s.at[0, n], recv_sem=r.at[0, n], device_id=(dp, partner), device_id_type=MESH)

    def rs_cross(xsend, xrec, s, r, n):
        return pltpu.make_async_remote_copy(src_ref=xsend.at[n], dst_ref=xrec.at[n], send_sem=s.at[1, n], recv_sem=r.at[1, n], device_id=(dp, cross), device_id_type=MESH)

    def rs_a(part, psend, prec, s, r, n):
        pf[...] = part.reshape(4, ROWS, PN)
        for q in range(2):
            psend[n, q] = pf[2 * q + other_core].astype(BF16)
            own[n, q] = pf[2 * q + core]
        rs_pair(psend, prec, s, r, n).start()

    def rs_b(psend, prec, xsend, xrec, s, r, n):
        rs_pair(psend, prec, s, r, n).wait_recv()
        xsend[n] = (own[n, other_chip] + prec[n, other_chip].astype(F32)).astype(BF16)
        rs_cross(xsend, xrec, s, r, n).start()
        xsum[n] = own[n, chip] + prec[n, chip].astype(F32)

    def rs_c(xsend, xrec, s, r, n):
        rs_cross(xsend, xrec, s, r, n).wait_recv()
        return xsum[n] + xrec[n].astype(F32)

    ctx_rows = ctx[...]

    def out_a(n):
        out_copy(n).wait()
        rs_a(jnp.dot(ctx_rows, slots[(G_OUT + n) % SLOTS], preferred_element_type=F32), psend1, prec1, rs1_s, rs1_r, n)
        g = G_OUT + n + SLOTS
        (up_copy(g - G_UP) if g < G_DOWN else down_copy(g - G_DOWN)).start()

    def out_b(n):
        rs_b(psend1, prec1, xsend1, xrec1, rs1_s, rs1_r, n)

    def ag2(which, block, peer, c):
        return push(x1_all, block, c, PK, ag2_s, ag2_r, which, peer)

    def st(which, block, peer):
        ref = stats.at[block]
        return pltpu.make_async_remote_copy(src_ref=ref, dst_ref=ref, send_sem=st_s.at[which], recv_sem=st_r.at[which], device_id=(dp, peer), device_id_type=MESH)

    lead = 3
    for n in range(NC):
        out_a(n)
        if n >= lead:
            out_b(n - lead)
    for n in range(NC - lead, NC):
        out_b(n)
    for n in range(NC):
        cols = slice(n * PN, (n + 1) * PN)
        total = rs_c(xsend1, xrec1, rs1_s, rs1_r, n)
        x1_all[me, :, cols] = (x_own[:, cols].astype(F32) + (total + rows[BOUT, :, cols])).astype(BF16)
        if n == NC - 2:
            ag2(0, me, cross, 0).start()
            ag2(1, me, partner, 0).start()
    for b in range(N_BATCH):
        r = pl.ds(b * BLOCK, BLOCK)
        mean, rstd = row_stats(x1_all[me, r, :].astype(F32))
        lane = lax.broadcasted_iota(jnp.int32, (BLOCK, 128), 1)
        square[r, :] = jnp.where(lane == 0, mean, rstd)
    stats[me] = square[...].T[:8]
    st(0, me, cross).start()
    st(2, me, far).start()
    st(1, me, partner).start()
    for c in range(1, KC):
        ag2(0, me, cross, c).start()
        ag2(1, me, partner, c).start()

    def ag2_forward(c):
        ag2(0, cross, cross, c).wait_recv()
        ag2(2, cross, partner, c).start()

    def arrive(c):
        ag2(1, partner, partner, c).wait_recv()
        ag2(2, far, partner, c).wait_recv()

    def normalize(c):
        cols = slice(c * PK, (c + 1) * PK)
        for d in range(4):
            xf = x1_all[d, :, cols].astype(F32)
            h_all[d, :, cols] = ((xf - stat_cols[d, :, 0:1]) * stat_cols[d, :, 1:2] * rows[G2, :, cols] + rows[B2, :, cols]).astype(BF16)

    def up_panels(c, panels):
        for n in panels:
            up_copy(c * NC + n).wait()
        h = tokens(h_all, c)
        for n in panels:
            wide = slice(n * PN, (n + 1) * PN)
            part = jnp.dot(h, slots[(G_UP + c * NC + n) % SLOTS], preferred_element_type=F32)
            if c:
                part = part + acc[:, wide]
            if c < KC - 1:
                acc[:, wide] = part
            else:
                u[:, wide] = jax.nn.gelu(part + rows[BUP, :, wide], approximate=True).astype(BF16)

    def refill(c, panels):
        for n in panels:
            i = c * NC + n + G_UP + SLOTS - G_DOWN
            if i < N_DOWN:
                down_copy(i).start()

    ag2_forward(0)
    st(1, partner, partner).wait_recv()
    st(0, cross, cross).wait_recv()
    st(2, far, far).wait_recv()
    for d in range(4):
        square[0:8, :] = stats[d]
        stat_cols[d] = square[...].T[:ROWS]
    arrive(0)
    normalize(0)
    for c in range(KC):
        up_panels(c, range(0, 4))
        refill(c, range(0, 4))
        if c < KC - 1:
            ag2_forward(c + 1)
            arrive(c + 1)
        up_panels(c, range(4, 8))
        if c < KC - 1:
            normalize(c + 1)
        refill(c, range(4, 8))

    def down_a(n):
        for k in range(KC):
            down_copy(n * KC + k).wait()
        part = None
        for k in range(KC):
            term = jnp.dot(u[:, k * PK:(k + 1) * PK], slots[(G_DOWN + n * KC + k) % SLOTS], preferred_element_type=F32)
            part = term if part is None else part + term
        rs_a(part, psend2, prec2, rs2_s, rs2_r, n)

    def down_b(n):
        rs_b(psend2, prec2, xsend2, xrec2, rs2_s, rs2_r, n)

    def down_c(n):
        cols = slice(n * PN, (n + 1) * PN)
        total = rs_c(xsend2, xrec2, rs2_s, rs2_r, n)
        out_ref[:, cols] = (x1_all[me, :, cols].astype(F32) + (total + rows[BDOWN, :, cols])).astype(BF16)

    for n in range(NC):
        down_a(n)
        if n >= 1:
            down_b(n - 1)
    down_b(NC - 1)
    for n in range(NC):
        down_c(n)

    for n in range(NC):
        rs_pair(psend1, prec1, rs1_s, rs1_r, n).wait_send()
        rs_cross(xsend1, xrec1, rs1_s, rs1_r, n).wait_send()
        rs_pair(psend2, prec2, rs2_s, rs2_r, n).wait_send()
        rs_cross(xsend2, xrec2, rs2_s, rs2_r, n).wait_send()
    for c in range(KC):
        ag2(0, me, cross, c).wait_send()
        ag2(1, me, partner, c).wait_send()
        ag2(2, cross, partner, c).wait_send()
    st(0, me, cross).wait_send()
    st(1, me, partner).wait_send()
    st(2, me, far).wait_send()


def solution(mesh):
    def device_body(hidden, ln1_gain, ln1_bias, w_qkv, b_qkv, w_out, b_out, ln2_gain, ln2_bias, w_up, b_up, w_down, b_down):
        args = (hidden.reshape(ROWS, D), ln1_gain.reshape(32, 128), ln1_bias.reshape(32, 128), w_qkv, b_qkv, w_out.reshape(HEADS * HEAD_DIM, D),
                b_out.reshape(32, 128), ln2_gain.reshape(32, 128), ln2_bias.reshape(32, 128), w_up, b_up.reshape(32, 128), w_down, b_down.reshape(32, 128))
        hbm = pl.BlockSpec(memory_space=pltpu.HBM)
        dma = pltpu.SemaphoreType.DMA
        rs_buffers = [pltpu.VMEM((NC, 2, ROWS, PN), BF16), pltpu.VMEM((NC, 2, ROWS, PN), BF16), pltpu.VMEM((NC, ROWS, PN), BF16), pltpu.VMEM((NC, ROWS, PN), BF16)]
        result = pl.pallas_call(
            kernel,
            out_shape=pltpu.VMEM((ROWS, D), BF16),
            in_specs=[hbm] * len(args),
            out_specs=pl.BlockSpec(memory_space=pltpu.VMEM),
            scratch_shapes=[
                pltpu.VMEM((STAGES, STAGE_ROWS, 3, HEADS, HEAD_DIM), BF16),
                pltpu.VMEM((SLOTS, PK, PN), BF16),
                pltpu.VMEM((ROWS, D), BF16),
                pltpu.VMEM((4, ROWS, D), BF16),
                pltpu.VMEM((4, ROWS, D), BF16),
                pltpu.VMEM((TOKENS, FF), F32),
                pltpu.VMEM((TOKENS, QKV), BF16),
                pltpu.VMEM((TOKENS, HEADS * HEAD_DIM), BF16),
                pltpu.VMEM((TOKENS, FF), BF16),
                pltpu.VMEM((NC, 2, ROWS, PN), F32),
                pltpu.VMEM((4, ROWS, PN), F32),
                *rs_buffers,
                *rs_buffers,
                pltpu.VMEM((NC, ROWS, PN), F32),
                pltpu.VMEM((4, 8, 128), F32),
                pltpu.VMEM((4, ROWS, 128), F32),
                pltpu.VMEM((128, 128), F32),
                pltpu.VMEM((4, 32, 128), F32),
                pltpu.VMEM((3, 32, 128), BF16),
                pltpu.VMEM((3, HEADS, HEAD_DIM), BF16),
                pltpu.VMEM((7, 1, D), F32),
                pltpu.VMEM((1, QKV), F32),
                pltpu.VMEM((TOKENS, TOKENS), F32),
                dma((STAGES,)), dma((SLOTS,)), dma((8,)), dma((1,)),
                dma((3, KC)), dma((3, KC)), dma((3, KC)), dma((3, KC)), dma((3,)), dma((3,)),
                dma((2, NC)), dma((2, NC)), dma((2, NC)), dma((2, NC)),
            ],
            compiler_params=pltpu.CompilerParams(collective_id=0, has_side_effects=True, vmem_limit_bytes=62 * 2**20),
            name="decoder_layer",
        )(*args)
        return result.reshape(hidden.shape)

    in_layout = (P("dp", "tp", None), P(), P(), P(None, None, "tp", None), P(None, "tp", None), P("tp", None, None), P(), P(), P(), P(None, "tp"), P("tp"), P("tp", None), P())
    return jax.shard_map(device_body, mesh=mesh, in_specs=in_layout, out_specs=P("dp", "tp", None), check_vma=False)
```

time: 73.1 us -> 65.5 us (0.90)
  Pallas kernels: 71.1 us -> 64.4 us
  local copies, waits for them, and re-layouts: 1.77 us -> 0.75 us
    pallas_call x1, Pallas kernels: 71.1 us -> 64.4 us  [device_body(): pl.pallas_call(kernel, out_shape=pltpu.VMEM((ROWS, D), BF16), in_specs=[h...]
    unnamed x1, local copies, waits for them, and re-layouts: 1.77 us -> 0.75 us
where the time goes in v2:
time: 65.5 us; the launch traced here: 65.2 us
  Pallas kernels  64.4 us (98%)
  local copies, waits for them, and re-layouts  0.75 us (1%)
    pallas_call x1, Pallas kernels, device_body(): pl.pallas_call(kernel, out_shape=pltpu.VMEM((ROWS, D), BF16), in_specs=[h...  64.4 us

profile of v2, /device:TPU:0, one launch (start us, length us, event | category | flops | bytes accessed | tf_op | source)
XLA Modules:
  0.0 65.2 jit_solution(12931287887863828761)
XLA Ops:
  0.0 64.4 %decoder_layer.1 = bf16[48,4096]{1,0:T(8,128)(2,1)S(1)} custom-call(bf16[48,4096]{1,0:T(8,128)(2,1)} %bitcast.12, f32[32,128]{1,0:T(8,128)} %bitcast.13, f32[32,128]{1,0:T(8,128)} %bitcast.14, bf16[4096,3,8,128]{3,2,1,0:T(8,128)(2,1)} %wqkv_hbm.1, bf16[3,8,128]{2,1,0:T(8,128)(2,1)} %bqkv_hbm.1, bf16[1024,4096]{1,0:T(8,128)(2,1)} %bitcast.11, ...), custom_call_target="tpu_custom_call" | custom-call | tf_op jit(solution)/shard_map/decoder_layer/pallas_call | solution.py:380
  64.4 0.7 %copy.15 = bf16[3,16,4096]{2,1,0:T(8,128)(2,1)} copy(bf16[3,16,4096]{2,1,0:T(8,128)(2,1)S(1)} %bitcast.10) | data formatting | bytes 786432

commit v3 on v2

--- a/solution.py
+++ b/solution.py
@@ -110,6 +110,34 @@
     for c in range(KC):
         ag1(1, me, partner, c).start()
 
+    def ag1_forward(c):
+        ag1(0, cross, cross, c).wait_recv()
+        ag1(2, cross, partner, c).start()
+
+    def relayout(i):
+        s = lax.rem(i, STAGES)
+        k, off = lax.div(i, 4), lax.rem(i, 4)
+        r = pl.ds(pl.multiple_of(off * STAGE_ROWS, STAGE_ROWS), STAGE_ROWS)
+        for t in range(3):
+            w = stage[s, :, t].reshape(STAGE_ROWS, HEADS * HEAD_DIM)
+            slots[k * 6 + 2 * t, r, :] = w[:, :PN]
+            slots[k * 6 + 2 * t + 1, r, :] = w[:, PN:]
+
+    def relayout_step(i, carry):
+        stage_copy(i).wait()
+        relayout(i)
+
+        @pl.when(i + STAGES < STEPS)
+        def _():
+            stage_copy(i + STAGES).start()
+
+        return carry
+
+    lax.fori_loop(0, STEPS - STAGES, relayout_step, 0)
+    for n in range(N_OUT):
+        out_copy(n).start()
+    for i in range(SLOTS - G_UP):
+        up_copy(i).start()
     for c in smalls[2:]:
         c.wait()
     for i in (G2, B2):
@@ -134,34 +162,8 @@
     square[...] = jnp.zeros_like(square)
     mask[...] = ((q_seq == k_seq) & (q_pos >= k_pos)).astype(F32)
 
-    def ag1_forward(c):
-        ag1(0, cross, cross, c).wait_recv()
-        ag1(2, cross, partner, c).start()
-
-    def relayout(i):
-        s = lax.rem(i, STAGES)
-        k, off = lax.div(i, 4), lax.rem(i, 4)
-        r = pl.ds(pl.multiple_of(off * STAGE_ROWS, STAGE_ROWS), STAGE_ROWS)
-        for t in range(3):
-            w = stage[s, :, t].reshape(STAGE_ROWS, HEADS * HEAD_DIM)
-            slots[k * 6 + 2 * t, r, :] = w[:, :PN]
-            slots[k * 6 + 2 * t + 1, r, :] = w[:, PN:]
-
-    def relayout_step(i, carry):
-        stage_copy(i).wait()
-        relayout(i)
-
-        @pl.when(i + STAGES < STEPS)
-        def _():
-            stage_copy(i + STAGES).start()
-
-        return carry
-
-    lax.fori_loop(0, STEPS - STAGES, relayout_step, 0)
-    for n in range(N_OUT):
-        out_copy(n).start()
-    for i in range(SLOTS - G_UP):
-        up_copy(i).start()
+    ag1_forward(0)
+    ag1_forward(1)
     lax.fori_loop(STEPS - STAGES, STEPS, relayout_step, 0)
 
     def tokens(buf, c):
@@ -183,9 +185,8 @@
         for n in range(6):
             up_copy(c * 6 + n + SLOTS - G_UP).start()
 
-    ag1_forward(0)
-    for c in range(KC):
-        if c < KC - 1:
+    for c in range(KC):
+        if 1 <= c < KC - 1:
             ag1_forward(c + 1)
         qkv_chunk(c)
     for c in range(KC):
@@ -261,7 +262,7 @@
         cols = slice(n * PN, (n + 1) * PN)
         total = rs_c(xsend1, xrec1, rs1_s, rs1_r, n)
         x1_all[me, :, cols] = (x_own[:, cols].astype(F32) + (total + rows[BOUT, :, cols])).astype(BF16)
-        if n == NC - 2:
+        if n == 1:
             ag2(0, me, cross, 0).start()
             ag2(1, me, partner, 0).start()
     for b in range(N_BATCH):
@@ -321,15 +322,18 @@
     arrive(0)
     normalize(0)
     for c in range(KC):
-        up_panels(c, range(0, 4))
-        refill(c, range(0, 4))
+        up_panels(c, range(0, 3))
+        refill(c, range(0, 3))
         if c < KC - 1:
             ag2_forward(c + 1)
+        up_panels(c, range(3, 7))
+        refill(c, range(3, 7))
+        if c < KC - 1:
             arrive(c + 1)
-        up_panels(c, range(4, 8))
+        up_panels(c, range(7, 8))
         if c < KC - 1:
             normalize(c + 1)
-        refill(c, range(4, 8))
+        refill(c, range(7, 8))
 
     def down_a(n):
         for k in range(KC):

time: 65.5 us -> 60.9 us (0.930)
  Pallas kernels: 64.4 us -> 60 us
    pallas_call x1, Pallas kernels: 64.4 us -> 60 us  [device_body(): pl.pallas_call(kernel, out_shape=pltpu.VMEM((ROWS, D), BF16), in_specs=[h...]
where the time goes in v3:
time: 60.9 us; the launch traced here: 60.8 us
  Pallas kernels  60 us (99%)
  local copies, waits for them, and re-layouts  0.75 us (1%)
    pallas_call x1, Pallas kernels, device_body(): pl.pallas_call(kernel, out_shape=pltpu.VMEM((ROWS, D), BF16), in_specs=[h...  60 us

profile of v3, /device:TPU:0, one launch (start us, length us, event | category | flops | bytes accessed | tf_op | source)
XLA Modules:
  0.0 60.8 jit_solution(6665751834560136671)
XLA Ops:
  0.0 60.0 %decoder_layer.1 = bf16[48,4096]{1,0:T(8,128)(2,1)S(1)} custom-call(bf16[48,4096]{1,0:T(8,128)(2,1)} %bitcast.12, f32[32,128]{1,0:T(8,128)} %bitcast.13, f32[32,128]{1,0:T(8,128)} %bitcast.14, bf16[4096,3,8,128]{3,2,1,0:T(8,128)(2,1)} %wqkv_hbm.1, bf16[3,8,128]{2,1,0:T(8,128)(2,1)} %bqkv_hbm.1, bf16[1024,4096]{1,0:T(8,128)(2,1)} %bitcast.11, ...), custom_call_target="tpu_custom_call" | custom-call | tf_op jit(solution)/shard_map/decoder_layer/pallas_call | solution.py:384
  60.0 0.7 %copy.15 = bf16[3,16,4096]{2,1,0:T(8,128)(2,1)} copy(bf16[3,16,4096]{2,1,0:T(8,128)(2,1)S(1)} %bitcast.10) | data formatting | bytes 786432

commit v4 on v0

v4 whole, which is shorter than its diff:
```python
import math

import jax
import jax.numpy as jnp
from jax import lax
from jax.experimental import pallas as pl
from jax.experimental.pallas import tpu as pltpu
from jax.sharding import PartitionSpec as P

MESH = pl.DeviceIdType.MESH
F32, BF16 = jnp.float32, jnp.bfloat16

LN_EPS = 1e-5
N_BATCH, BLOCK, D = 3, 16, 4096
ROWS = N_BATCH * BLOCK
TOKENS = 4 * ROWS
HEADS, HEAD_DIM = 8, 128
FF = 4096
QKV = 3 * HEADS * HEAD_DIM

PK, PN = 1024, 512
NK, NN = D // PK, D // PN
AG1_CHUNKS = [(k * PK, PK) for k in range(NK)]
AG2_CHUNKS = [(0, 1024), (1024, 1024), (2048, 1024), (3072, 512), (3584, 512)]
RS_CHUNKS = [(n * PN, PN) for n in range(NN)]
RING = 9
G_OUT, G_UP, G_DOWN, G_END = 6, 8, 16, 24
STAGE_ROWS, STAGES = 256, 4
STEPS = D // STAGE_ROWS


def kernel(x_hbm, g1_hbm, b1_hbm, wqkv_hbm, bqkv_hbm, wout_hbm, bout_hbm, g2_hbm, b2_hbm, wup_hbm, bup_hbm, wdown_hbm, bdown_hbm, out_ref,
           stage, x_own, h_all, x1_all, h2_even, h2_odd, acc, qkv_bf, ctx, u,
           psend1, prec1, xsend1, xrec1, psend2, prec2, xsend2, xrec2, stats, stat_cols, square,
           vec_f32, vec_bf, bqkv_v, rows, bqkv_row, mask,
           stage_sem, ring_sem, small_sem, send_sem, gather_sem, st_sem, rs_sem, *ring):
    dp = lax.axis_index("dp")
    me = lax.axis_index("tp")
    core = lax.rem(me, 2)
    chip = lax.div(me, 2)
    partner = me + 1 - 2 * core
    cross = lax.rem(me + 2, 4)
    far = lax.rem(partner + 2, 4)
    other_core = 1 - core
    other_chip = 1 - chip
    SEND_AG1, SEND_AG2, SEND_ST, SEND_RS1, SEND_RS2 = 0, 1, 2, 3, 5

    def remote(src, dst, send, recv, peer):
        return pltpu.make_async_remote_copy(src_ref=src, dst_ref=dst, send_sem=send, recv_sem=recv, device_id=(dp, peer), device_id_type=MESH)

    def stage_copy(i):
        return pltpu.make_async_copy(wqkv_hbm.at[pl.ds(i * STAGE_ROWS, STAGE_ROWS)], stage.at[lax.rem(i, STAGES)], stage_sem.at[lax.rem(i, STAGES)])

    def load_group(g):
        to, sem = ring[g % RING], ring_sem.at[g % RING]
        if g >= G_END:
            return
        if g >= G_DOWN:
            pltpu.make_async_copy(wdown_hbm.at[:, :, pl.ds((g - G_DOWN) * PN, PN)], to, sem).start()
            return
        for m in range(4):
            if g >= G_UP:
                k, n = (g - G_UP) // 2, (g - G_UP) % 2 * 4 + m
                src = wup_hbm.at[pl.ds(k * PK, PK), pl.ds(n * PN, PN)]
            else:
                src = wout_hbm.at[:, pl.ds(((g - G_OUT) * 4 + m) * PN, PN)]
            pltpu.make_async_copy(src, to.at[m], sem).start()

    def await_group(g):
        pltpu.make_async_copy(wdown_hbm.at[:, :, pl.ds(0, PN)], ring[g % RING], ring_sem.at[g % RING]).wait()

    barrier = pltpu.get_barrier_semaphore()
    for peer in (partner, cross, far):
        pl.semaphore_signal(barrier, inc=1, device_id=(dp, peer), device_id_type=MESH)
    G1, B1, G2, B2, BOUT, BUP, BDOWN = range(7)
    x_copy = pltpu.make_async_copy(x_hbm, x_own, small_sem.at[4])
    for i, src in enumerate((g1_hbm, b1_hbm)):
        pltpu.make_async_copy(src, vec_f32.at[i], small_sem.at[0]).start()
    x_copy.start()
    stage_copy(0).start()

    def f32_row(i):
        for j in range(32):
            rows[i, :, j * 128:(j + 1) * 128] = vec_f32[i, j:j + 1, :]

    def row_stats(x):
        mean = jnp.mean(x, axis=-1, keepdims=True)
        centered = x - mean
        var = jnp.mean(centered * centered, axis=-1, keepdims=True)
        return mean, lax.rsqrt(var + LN_EPS)

    pltpu.make_async_copy(vec_f32.at[pl.ds(2, 2)], vec_f32.at[pl.ds(0, 2)], small_sem.at[0]).wait()
    for i in (G1, B1):
        f32_row(i)
    x_copy.wait()
    for i in range(1, STAGES):
        stage_copy(i).start()
    for i, src in enumerate((g2_hbm, b2_hbm)):
        pltpu.make_async_copy(src, vec_f32.at[2 + i], small_sem.at[1]).start()
    for i, src in enumerate((bout_hbm, bup_hbm, bdown_hbm)):
        pltpu.make_async_copy(src, vec_bf.at[i], small_sem.at[2]).start()
    bqkv_copy = pltpu.make_async_copy(bqkv_hbm, bqkv_v, small_sem.at[3])
    bqkv_copy.start()
    for b in range(N_BATCH):
        r = pl.ds(b * BLOCK, BLOCK)
        xf = x_own[r, :].astype(F32)
        mean, rstd = row_stats(xf)
        h_all[me, r, :] = ((xf - mean) * rstd * rows[G1] + rows[B1]).astype(BF16)

    pl.semaphore_wait(barrier, 3)

    PARTNER, CROSS, FAR = range(3)

    def push(buf, chunks, send, which, block, peer, c):
        ref = buf.at[block, :, pl.ds(*chunks[c])]
        return remote(ref, ref, send_sem.at[send], gather_sem.at[which, c], peer)

    def ag1(which, block, peer, c):
        return push(h_all, AG1_CHUNKS, SEND_AG1, which, block, peer, c)

    def ag1_partner(block):
        return remote(h_all.at[block], h_all.at[block], send_sem.at[SEND_AG1], gather_sem.at[PARTNER, 0], partner)

    for c in range(NK):
        ag1(CROSS, me, cross, c).start()
    ag1_partner(me).start()

    def ag1_forward(c):
        ag1(CROSS, cross, cross, c).wait_recv()
        ag1(FAR, cross, partner, c).start()

    def relayout(k, off):
        s = lax.rem(k * 4 + off, STAGES)
        r = pl.ds(pl.multiple_of(off * STAGE_ROWS, STAGE_ROWS), STAGE_ROWS)
        for t in range(3):
            w = stage[s, :, t].reshape(STAGE_ROWS, HEADS * HEAD_DIM)
            for half in range(2):
                p = k * 6 + 2 * t + half
                ring[p // 4][p % 4, r, :] = w[:, half * PN:(half + 1) * PN]

    def relayout_chunk(k):
        def step(off, carry):
            stage_copy(k * 4 + off).wait()
            relayout(k, off)
            if k < NK - 1:
                stage_copy(k * 4 + off + STAGES).start()
            return carry

        lax.fori_loop(0, 4, step, 0)

    for k in range(3):
        relayout_chunk(k)
    pltpu.make_async_copy(vec_f32.at[pl.ds(0, 2)], vec_f32.at[pl.ds(2, 2)], small_sem.at[1]).wait()
    pltpu.make_async_copy(vec_bf, vec_bf, small_sem.at[2]).wait()
    bqkv_copy.wait()
    for i in (G2, B2):
        f32_row(i)
    for i in range(3):
        vals = vec_bf[i].astype(F32)
        for j in range(32):
            rows[4 + i, :, j * 128:(j + 1) * 128] = vals[j:j + 1, :]
    for t in range(3):
        vals = bqkv_v[t].astype(F32)
        for j in range(HEADS):
            bqkv_row[:, (t * HEADS + j) * 128:(t * HEADS + j + 1) * 128] = vals[j:j + 1, :]

    def token_place(axis):
        t = lax.broadcasted_iota(jnp.int32, (TOKENS, TOKENS), axis)
        d = sum((t >= ROWS * i).astype(jnp.int32) for i in range(1, 4))
        t = t - ROWS * d
        b = sum((t >= BLOCK * i).astype(jnp.int32) for i in range(1, N_BATCH))
        return b, d * BLOCK + t - BLOCK * b

    (q_seq, q_pos), (k_seq, k_pos) = token_place(0), token_place(1)
    square[...] = jnp.zeros_like(square)
    mask[...] = ((q_seq == k_seq) & (q_pos >= k_pos)).astype(F32)
    ag1_forward(0)
    ag1_forward(1)
    relayout_chunk(3)
    for g in range(G_OUT, RING):
        load_group(g)
    def all_rows(ref, start, size):
        return ref[:, :, start:start + size].reshape(TOKENS, size)

    def qkv_chunk(c):
        ag1(FAR, far, partner, c).wait_recv()
        h = all_rows(h_all, *AG1_CHUNKS[c])
        for n in range(6):
            p = c * 6 + n
            part = jnp.dot(h, ring[p // 4][p % 4], preferred_element_type=F32)
            if c:
                part = part + all_rows(acc, n * PN, PN)
            if c < NK - 1:
                acc[:, :, n * PN:(n + 1) * PN] = part.reshape(4, ROWS, PN)
            else:
                qkv_bf[:, n * PN:(n + 1) * PN] = (part + bqkv_row[:, n * PN:(n + 1) * PN]).astype(BF16)
        for g in range(c * 6 // 4, (c + 1) * 6 // 4):
            load_group(g + RING)

    ag1_partner(partner).wait_recv()
    for c in range(NK):
        if c + 2 < NK:
            ag1_forward(c + 2)
        qkv_chunk(c)

    keep = mask[...] > 0.5
    for first in range(0, HEADS, 4):
        heads = range(first, first + 4)

        def part_of(t, j):
            return qkv_bf[:, (t * HEADS + j) * HEAD_DIM:(t * HEADS + j + 1) * HEAD_DIM]

        logits = [lax.dot_general(part_of(0, j), part_of(1, j), (((1,), (1,)), ((), ())), preferred_element_type=F32) for j in heads]
        logits = [jnp.where(keep, x * HEAD_DIM ** -0.5, -1e30) for x in logits]
        tops = [jnp.max(x, axis=-1, keepdims=True) for x in logits]
        es = [jnp.exp(x - t) for x, t in zip(logits, tops)]
        sums = [jnp.sum(e, axis=-1, keepdims=True) for e in es]
        ps = [(e * (1.0 / z)).astype(BF16) for e, z in zip(es, sums)]
        for j, p in zip(heads, ps):
            ctx[:, j * HEAD_DIM:(j + 1) * HEAD_DIM] = jnp.dot(p, part_of(2, j), preferred_element_type=F32).astype(BF16)

    def reduction(psend, prec, xsend, xrec, send):
        def pair(n):
            at = (slice(None), slice(None), pl.ds(*RS_CHUNKS[n]))
            return remote(psend.at[at], prec.at[at], send_sem.at[send], rs_sem.at[0, n], partner)

        def across(n):
            at = (slice(None), pl.ds(*RS_CHUNKS[n]))
            return remote(xsend.at[at], xrec.at[at], send_sem.at[send + 1], rs_sem.at[1, n], cross)

        def to_pair(n, part):
            cols = pl.ds(*RS_CHUNKS[n])
            acc[:, :, cols] = part.reshape(4, ROWS, RS_CHUNKS[n][1])
            for q in range(2):
                psend[q, :, cols] = acc[2 * q + other_core, :, cols].astype(BF16)
            pair(n).start()

        def to_cross(n):
            cols = pl.ds(*RS_CHUNKS[n])
            pair(n).wait_recv()
            xsend[:, cols] = (acc[2 * other_chip + core, :, cols] + prec[other_chip, :, cols].astype(F32)).astype(BF16)
            across(n).start()

        def total(n):
            cols = pl.ds(*RS_CHUNKS[n])
            across(n).wait_recv()
            return acc[me, :, cols] + prec[chip, :, cols].astype(F32) + xrec[:, cols].astype(F32)

        def drain():
            remote(psend, prec, send_sem.at[send], rs_sem.at[0, 0], partner).wait_send()
            remote(xsend, xrec, send_sem.at[send + 1], rs_sem.at[1, 0], cross).wait_send()

        return to_pair, to_cross, total, drain

    NR = len(RS_CHUNKS)
    rs1_pair, rs1_cross, rs1_total, rs1_drain = reduction(psend1, prec1, xsend1, xrec1, SEND_RS1)
    rs2_pair, rs2_cross, rs2_total, rs2_drain = reduction(psend2, prec2, xsend2, xrec2, SEND_RS2)

    def ag2(which, block, peer, c):
        return push(x1_all, AG2_CHUNKS, SEND_AG2, which, block, peer, c)

    def st(block, peer):
        return remote(stats.at[block], stats.at[block], send_sem.at[SEND_ST], st_sem.at[0], peer)

    ctx_rows = ctx[...]
    lead = 2
    for g in range(G_OUT, G_UP):
        await_group(g)
    for n, (start, size) in enumerate(RS_CHUNKS):
        g, m = G_OUT + start // PN // 4, start // PN % 4
        rs1_pair(n, jnp.dot(ctx_rows, ring[g % RING][m, :, start % PN:start % PN + size], preferred_element_type=F32))
        if n >= lead:
            rs1_cross(n - lead)
    for g in range(G_OUT, G_UP):
        load_group(g + RING)
    for n in range(NR - lead, NR):
        rs1_cross(n)
    for n, (start, size) in enumerate(RS_CHUNKS):
        cols = pl.ds(start, size)
        x1_all[me, :, cols] = (x_own[:, cols].astype(F32) + (rs1_total(n) + rows[BOUT, :, cols])).astype(BF16)
        if start + size == sum(AG2_CHUNKS[0]):
            ag2(CROSS, me, cross, 0).start()
            ag2(PARTNER, me, partner, 0).start()
    for b in range(N_BATCH):
        r = pl.ds(b * BLOCK, BLOCK)
        mean, rstd = row_stats(x1_all[me, r, :].astype(F32))
        lane = lax.broadcasted_iota(jnp.int32, (BLOCK, 128), 1)
        square[r, :] = jnp.where(lane == 0, mean, rstd)
    stats[me] = square[...].T[:8]
    for peer in (cross, far, partner):
        st(me, peer).start()
    for c in range(1, len(AG2_CHUNKS)):
        ag2(CROSS, me, cross, c).start()
        ag2(PARTNER, me, partner, c).start()

    def ag2_forward(c):
        ag2(CROSS, cross, cross, c).wait_recv()
        ag2(FAR, cross, partner, c).start()

    def normalize(c, blocks):
        start, size = AG2_CHUNKS[c]
        cols = pl.ds(start, size)
        to = (h2_even, h2_odd)[c % 2]
        for d in blocks:
            xf = x1_all[d, :, cols].astype(F32)
            to[d, :, 0:size] = ((xf - stat_cols[d, :, 0:1]) * stat_cols[d, :, 1:2] * rows[G2, :, cols] + rows[B2, :, cols]).astype(BF16)

    def gelu(x):
        scale = (2 / math.pi) ** 0.5
        halved = 0.5 * x
        return halved + halved * jnp.tanh(x * (scale + (scale * 0.044715) * (x * x)))

    def up_half(c, half):
        start, size = AG2_CHUNKS[c]
        h = all_rows((h2_even, h2_odd)[c % 2], 0, size)
        g = G_UP + start // PK * 2 + half
        for m in range(4):
            n = half * 4 + m
            part = jnp.dot(h, ring[g % RING][m, start % PK:start % PK + size, :], preferred_element_type=F32)
            part = part + (all_rows(acc, n * PN, PN) if c else rows[BUP, :, n * PN:(n + 1) * PN])
            if c < len(AG2_CHUNKS) - 1:
                acc[:, :, n * PN:(n + 1) * PN] = part.reshape(4, ROWS, PN)
            else:
                u[:, n * PN:(n + 1) * PN] = gelu(part).astype(BF16)

    def down_sum(n):
        total = None
        for k in range(NK):
            term = jnp.dot(u[:, k * PK:(k + 1) * PK], ring[(G_DOWN + n) % RING][k], preferred_element_type=F32)
            total = term if total is None else total + term
        return total

    ag2_forward(0)
    remote(stats.at[pl.ds(0, 3)], stats.at[pl.ds(0, 3)], send_sem.at[SEND_ST], st_sem.at[0], partner).wait_recv()
    for d in range(4):
        square[0:8, :] = stats[d]
        stat_cols[d] = square[...].T[:ROWS]
    ag2(PARTNER, partner, partner, 0).wait_recv()
    ag2(FAR, far, partner, 0).wait_recv()
    normalize(0, range(4))
    for c, (start, size) in enumerate(AG2_CHUNKS[:-1]):
        g = G_UP + start // PK * 2
        if start % PK == 0:
            await_group(g)
            await_group(g + 1)
        up_half(c, 0)
        ag2_forward(c + 1)
        ag2(PARTNER, partner, partner, c + 1).wait_recv()
        normalize(c + 1, (me, partner, cross))
        up_half(c, 1)
        if (start + size) % PK == 0:
            load_group(g + RING)
            load_group(g + 1 + RING)
        ag2(FAR, far, partner, c + 1).wait_recv()
        normalize(c + 1, (far,))

    await_group(G_DOWN)
    for half in range(2):
        up_half(len(AG2_CHUNKS) - 1, half)
    rs2_pair(0, down_sum(0))
    load_group(G_DOWN - 2 + RING)
    load_group(G_DOWN - 1 + RING)
    for n in range(1, NR):
        await_group(G_DOWN + n)
        rs2_pair(n, down_sum(n))
        rs2_cross(n - 1)
    rs2_cross(NR - 1)
    for n, (start, size) in enumerate(RS_CHUNKS):
        cols = pl.ds(start, size)
        out_ref[:, cols] = (x1_all[me, :, cols].astype(F32) + (rs2_total(n) + rows[BDOWN, :, cols])).astype(BF16)

    for buf, send in ((h_all, SEND_AG1), (x1_all, SEND_AG2), (stats, SEND_ST)):
        remote(buf.at[pl.ds(0, 3)], buf.at[pl.ds(0, 3)], send_sem.at[send], st_sem.at[0], partner).wait_send()
    rs1_drain()
    rs2_drain()


def solution(mesh):
    def device_body(hidden, ln1_gain, ln1_bias, w_qkv, b_qkv, w_out, b_out, ln2_gain, ln2_bias, w_up, b_up, w_down, b_down):
        args = (hidden.reshape(ROWS, D), ln1_gain.reshape(32, 128), ln1_bias.reshape(32, 128), w_qkv, b_qkv, w_out.reshape(HEADS * HEAD_DIM, D),
                b_out.reshape(32, 128), ln2_gain.reshape(32, 128), ln2_bias.reshape(32, 128), w_up, b_up.reshape(32, 128), w_down.reshape(NK, PK, D), b_down.reshape(32, 128))
        hbm = pl.BlockSpec(memory_space=pltpu.HBM)
        dma = pltpu.SemaphoreType.DMA
        rs_buffers = [pltpu.VMEM((2, ROWS, D), BF16), pltpu.VMEM((2, ROWS, D), BF16), pltpu.VMEM((ROWS, D), BF16), pltpu.VMEM((ROWS, D), BF16)]
        result = pl.pallas_call(
            kernel,
            out_shape=pltpu.VMEM((ROWS, D), BF16),
            in_specs=[hbm] * len(args),
            out_specs=pl.BlockSpec(memory_space=pltpu.VMEM),
            scratch_shapes=[
                pltpu.VMEM((STAGES, STAGE_ROWS, 3, HEADS, HEAD_DIM), BF16),
                pltpu.VMEM((ROWS, D), BF16),
                pltpu.VMEM((4, ROWS, D), BF16),
                pltpu.VMEM((4, ROWS, D), BF16),
                pltpu.VMEM((4, ROWS, PK), BF16),
                pltpu.VMEM((4, ROWS, PK), BF16),
                pltpu.VMEM((4, ROWS, FF), F32),
                pltpu.VMEM((TOKENS, QKV), BF16),
                pltpu.VMEM((TOKENS, HEADS * HEAD_DIM), BF16),
                pltpu.VMEM((TOKENS, FF), BF16),
                *rs_buffers,
                *rs_buffers,
                pltpu.VMEM((4, 8, 128), F32),
                pltpu.VMEM((4, ROWS, 128), F32),
                pltpu.VMEM((128, 128), F32),
                pltpu.VMEM((4, 32, 128), F32),
                pltpu.VMEM((3, 32, 128), BF16),
                pltpu.VMEM((3, HEADS, HEAD_DIM), BF16),
                pltpu.VMEM((7, 1, D), F32),
                pltpu.VMEM((1, QKV), F32),
                pltpu.VMEM((TOKENS, TOKENS), F32),
                dma((STAGES,)), dma((RING,)), dma((5,)), dma((7,)), dma((3, len(AG2_CHUNKS))), dma((1,)), dma((2, len(RS_CHUNKS))),
                *[pltpu.VMEM((4, PK, PN), BF16)] * RING,
            ],
            compiler_params=pltpu.CompilerParams(collective_id=0, has_side_effects=True, vmem_limit_bytes=62 * 2**20),
            name="decoder_layer",
        )(*args)
        return result.reshape(hidden.shape)

    in_layout = (P("dp", "tp", None), P(), P(), P(None, None, "tp", None), P(None, "tp", None), P("tp", None, None), P(), P(), P(), P(None, "tp"), P("tp"), P("tp", None), P())
    return jax.shard_map(device_body, mesh=mesh, in_specs=in_layout, out_specs=P("dp", "tp", None), check_vma=False)
```

time: 152 us -> 58.6 us (0.39)
  waiting for transfers between devices: 75.2 us -> 0 us
  Pallas kernels: 0 us -> 57.7 us
  matrix products: 44.2 us -> 0 us
  between operations: 13.6 us -> 0.01 us
  other arithmetic: 8.65 us -> 0 us
  starting transfers between devices: 7.3 us -> 0 us
  local copies, waits for them, and re-layouts: 2.57 us -> 0.75 us
    pallas_call x0 -> x1, Pallas kernels: none -> 57.7 us  [device_body(): pl.pallas_call(kernel, out_shape=pltpu.VMEM((ROWS, D), BF16), in_specs=[h...]
    dot_general x4 -> x0, matrix products: 44.2 us -> none  [the longest x1 24.7 us: device_body(): jnp.einsum('bsf,fd->bsd', gelu_out, w_down, preferred_element_type=jnp.fl...]
    all_to_all x2 -> x0, waiting for transfers between devices: 39.5 us -> none  [scatter_sum(): received = lax.all_to_all(split_view, 'tp', 1, 1, tiled=True)]
    all_gather x2 -> x0, waiting for transfers between devices: 35.7 us -> none  [the longest x1 18.9 us: device_body(): normed_all = lax.all_gather(normed, 'tp', axis=1, tiled=True)]
    all_to_all x2 -> x0, starting transfers between devices: 7.25 us -> none  [scatter_sum(): received = lax.all_to_all(split_view, 'tp', 1, 1, tiled=True)]
    convert_element_type x7 -> x0, other arithmetic: 4.51 us -> none  [the longest x2 2.94 us: layer_norm(): (centered * lax.rsqrt(variance + LN_EPS) * gain_vec + shift_vec).astype(j...]
    reduce_sum x6 -> x0, other arithmetic: 3.29 us -> none  [the longest x2 1.48 us: layer_norm(): variance = jnp.mean(centered * centered, axis=-1, keepdims=True)]
    reshape x2 -> x0, local copies, waits for them, and re-layouts: 2.53 us -> none  [scatter_sum(): partial.astype(jnp.bfloat16)]
  transfers between devices with their start and end apart: 4 -> 0, of which waited for: 4 -> 0; matrix products, arithmetic and copies ran while one was open for 0% -> 0% of each run, Pallas kernels for 0% -> 0%
where the time goes in v4:
time: 58.6 us; the launch traced here: 58.5 us
  Pallas kernels  57.7 us (98%)
  local copies, waits for them, and re-layouts  0.75 us (1%)
    pallas_call x1, Pallas kernels, device_body(): pl.pallas_call(kernel, out_shape=pltpu.VMEM((ROWS, D), BF16), in_specs=[h...  57.7 us

profile of v4, /device:TPU:0, one launch (start us, length us, event | category | flops | bytes accessed | tf_op | source)
XLA Modules:
  0.0 58.5 jit_solution(12233271190541522450)
XLA Ops:
  0.0 57.7 %decoder_layer.1 = bf16[48,4096]{1,0:T(8,128)(2,1)S(1)} custom-call(bf16[48,4096]{1,0:T(8,128)(2,1)} %bitcast.14, f32[32,128]{1,0:T(8,128)} %bitcast.15, f32[32,128]{1,0:T(8,128)} %bitcast.16, bf16[4096,3,8,128]{3,2,1,0:T(8,128)(2,1)} %wqkv_hbm.1, bf16[3,8,128]{2,1,0:T(8,128)(2,1)} %bqkv_hbm.1, bf16[1024,4096]{1,0:T(8,128)(2,1)} %bitcast.13, ...), custom_call_target="tpu_custom_call" | custom-call | tf_op jit(solution)/shard_map/decoder_layer/pallas_call | solution.py:385
  57.7 0.7 %copy.15 = bf16[3,16,4096]{2,1,0:T(8,128)(2,1)} copy(bf16[3,16,4096]{2,1,0:T(8,128)(2,1)S(1)} %bitcast.11) | data formatting | bytes 786432

commit v5 on v4

--- a/solution.py
+++ b/solution.py
@@ -21,7 +21,7 @@
 PK, PN = 1024, 512
 NK, NN = D // PK, D // PN
 AG1_CHUNKS = [(k * PK, PK) for k in range(NK)]
-AG2_CHUNKS = [(0, 1024), (1024, 1024), (2048, 1024), (3072, 512), (3584, 512)]
+AG2_CHUNKS = [(0, 1024), (1024, 512), (1536, 1024), (2560, 1024), (3584, 512)]
 RS_CHUNKS = [(n * PN, PN) for n in range(NN)]
 RING = 9
 G_OUT, G_UP, G_DOWN, G_END = 6, 8, 16, 24
@@ -92,8 +92,9 @@
     pltpu.make_async_copy(vec_f32.at[pl.ds(2, 2)], vec_f32.at[pl.ds(0, 2)], small_sem.at[0]).wait()
     for i in (G1, B1):
         f32_row(i)
+    stage_copy(1).start()
     x_copy.wait()
-    for i in range(1, STAGES):
+    for i in range(2, STAGES):
         stage_copy(i).start()
     for i, src in enumerate((g2_hbm, b2_hbm)):
         pltpu.make_async_copy(src, vec_f32.at[2 + i], small_sem.at[1]).start()
@@ -182,26 +183,29 @@
     def all_rows(ref, start, size):
         return ref[:, :, start:start + size].reshape(TOKENS, size)
 
-    def qkv_chunk(c):
-        ag1(FAR, far, partner, c).wait_recv()
-        h = all_rows(h_all, *AG1_CHUNKS[c])
+    def qkv_block(chunks):
+        for c in chunks:
+            ag1(FAR, far, partner, c).wait_recv()
+        first, last = chunks[0] == 0, chunks[-1] == NK - 1
         for n in range(6):
-            p = c * 6 + n
-            part = jnp.dot(h, ring[p // 4][p % 4], preferred_element_type=F32)
-            if c:
-                part = part + all_rows(acc, n * PN, PN)
-            if c < NK - 1:
+            part = None if first else all_rows(acc, n * PN, PN)
+            for c in chunks:
+                p = c * 6 + n
+                term = jnp.dot(all_rows(h_all, *AG1_CHUNKS[c]), ring[p // 4][p % 4], preferred_element_type=F32)
+                part = term if part is None else part + term
+            if last:
+                qkv_bf[:, n * PN:(n + 1) * PN] = (part + bqkv_row[:, n * PN:(n + 1) * PN]).astype(BF16)
+            else:
                 acc[:, :, n * PN:(n + 1) * PN] = part.reshape(4, ROWS, PN)
-            else:
-                qkv_bf[:, n * PN:(n + 1) * PN] = (part + bqkv_row[:, n * PN:(n + 1) * PN]).astype(BF16)
-        for g in range(c * 6 // 4, (c + 1) * 6 // 4):
+        for g in range(chunks[0] * 6 // 4, (chunks[-1] + 1) * 6 // 4):
             load_group(g + RING)
 
     ag1_partner(partner).wait_recv()
-    for c in range(NK):
-        if c + 2 < NK:
-            ag1_forward(c + 2)
-        qkv_chunk(c)
+    ag1_forward(2)
+    qkv_block((0,))
+    ag1_forward(3)
+    qkv_block((1,))
+    qkv_block((2, 3))
 
     keep = mask[...] > 0.5
     for first in range(0, HEADS, 4):
@@ -277,15 +281,22 @@
         rs1_cross(n)
     for n, (start, size) in enumerate(RS_CHUNKS):
         cols = pl.ds(start, size)
-        x1_all[me, :, cols] = (x_own[:, cols].astype(F32) + (rs1_total(n) + rows[BOUT, :, cols])).astype(BF16)
+        x1 = (x_own[:, cols].astype(F32) + (rs1_total(n) + rows[BOUT, :, cols])).astype(BF16)
+        x1_all[me, :, cols] = x1
+        x1 = x1.astype(F32)
+        part_mean = jnp.mean(x1, axis=-1, keepdims=True)
+        part_dist = jnp.sum((x1 - part_mean) * (x1 - part_mean), axis=-1, keepdims=True)
+        if n == 0:
+            mean, dist = part_mean, part_dist
+        else:
+            step = part_mean - mean
+            mean = mean + step * (size / (start + size))
+            dist = dist + part_dist + step * step * (start * size / (start + size))
         if start + size == sum(AG2_CHUNKS[0]):
             ag2(CROSS, me, cross, 0).start()
             ag2(PARTNER, me, partner, 0).start()
-    for b in range(N_BATCH):
-        r = pl.ds(b * BLOCK, BLOCK)
-        mean, rstd = row_stats(x1_all[me, r, :].astype(F32))
-        lane = lax.broadcasted_iota(jnp.int32, (BLOCK, 128), 1)
-        square[r, :] = jnp.where(lane == 0, mean, rstd)
+    lane = lax.broadcasted_iota(jnp.int32, (ROWS, 128), 1)
+    square[0:ROWS, :] = jnp.where(lane == 0, mean, lax.rsqrt(dist * (1.0 / D) + LN_EPS))
     stats[me] = square[...].T[:8]
     for peer in (cross, far, partner):
         st(me, peer).start()
@@ -310,14 +321,20 @@
         halved = 0.5 * x
         return halved + halved * jnp.tanh(x * (scale + (scale * 0.044715) * (x * x)))
 
+    def blocks_of(c):
+        start, size = AG2_CHUNKS[c]
+        edges = sorted({start, start + size} | {k * PK for k in range(NK) if start < k * PK < start + size})
+        return [(lo // PK, lo % PK, hi - lo) for lo, hi in zip(edges, edges[1:])]
+
     def up_half(c, half):
-        start, size = AG2_CHUNKS[c]
-        h = all_rows((h2_even, h2_odd)[c % 2], 0, size)
-        g = G_UP + start // PK * 2 + half
-        for m in range(4):
-            n = half * 4 + m
-            part = jnp.dot(h, ring[g % RING][m, start % PK:start % PK + size, :], preferred_element_type=F32)
-            part = part + (all_rows(acc, n * PN, PN) if c else rows[BUP, :, n * PN:(n + 1) * PN])
+        h = all_rows((h2_even, h2_odd)[c % 2], 0, AG2_CHUNKS[c][1])
+        for n in range(half * 4, half * 4 + 4):
+            part, done = all_rows(acc, n * PN, PN) if c else rows[BUP, :, n * PN:(n + 1) * PN], 0
+            total = None
+            for k, row, size in blocks_of(c):
+                term = jnp.dot(h[:, done:done + size], ring[(G_UP + k * 2 + half) % RING][n % 4, row:row + size, :], preferred_element_type=F32)
+                total, done = term if total is None else total + term, done + size
+            part = total + part
             if c < len(AG2_CHUNKS) - 1:
                 acc[:, :, n * PN:(n + 1) * PN] = part.reshape(4, ROWS, PN)
             else:
@@ -338,19 +355,20 @@
     ag2(PARTNER, partner, partner, 0).wait_recv()
     ag2(FAR, far, partner, 0).wait_recv()
     normalize(0, range(4))
-    for c, (start, size) in enumerate(AG2_CHUNKS[:-1]):
-        g = G_UP + start // PK * 2
-        if start % PK == 0:
-            await_group(g)
-            await_group(g + 1)
+    for c in range(len(AG2_CHUNKS) - 1):
+        for k, row, size in blocks_of(c):
+            if row == 0:
+                await_group(G_UP + 2 * k)
+                await_group(G_UP + 2 * k + 1)
         up_half(c, 0)
         ag2_forward(c + 1)
         ag2(PARTNER, partner, partner, c + 1).wait_recv()
         normalize(c + 1, (me, partner, cross))
         up_half(c, 1)
-        if (start + size) % PK == 0:
-            load_group(g + RING)
-            load_group(g + 1 + RING)
+        for k, row, size in blocks_of(c):
+            if row + size == PK:
+                load_group(G_UP + 2 * k + RING)
+                load_group(G_UP + 2 * k + 1 + RING)
         ag2(FAR, far, partner, c + 1).wait_recv()
         normalize(c + 1, (far,))
 

time: 58.6 us -> 57.6 us (0.983)
  Pallas kernels: 57.7 us -> 56.7 us
    pallas_call x1, Pallas kernels: 57.7 us -> 56.7 us  [device_body(): pl.pallas_call(kernel, out_shape=pltpu.VMEM((ROWS, D), BF16), in_specs=[h...]
where the time goes in v5:
time: 57.6 us; the launch traced here: 57.5 us
  Pallas kernels  56.7 us (98%)
  local copies, waits for them, and re-layouts  0.75 us (1%)
    pallas_call x1, Pallas kernels, device_body(): pl.pallas_call(kernel, out_shape=pltpu.VMEM((ROWS, D), BF16), in_specs=[h...  56.7 us

profile of v5, /device:TPU:0, one launch (start us, length us, event | category | flops | bytes accessed | tf_op | source)
XLA Modules:
  0.0 57.5 jit_solution(7938155614543770125)
XLA Ops:
  0.0 56.7 %decoder_layer.1 = bf16[48,4096]{1,0:T(8,128)(2,1)S(1)} custom-call(bf16[48,4096]{1,0:T(8,128)(2,1)} %bitcast.14, f32[32,128]{1,0:T(8,128)} %bitcast.15, f32[32,128]{1,0:T(8,128)} %bitcast.16, bf16[4096,3,8,128]{3,2,1,0:T(8,128)(2,1)} %wqkv_hbm.1, bf16[3,8,128]{2,1,0:T(8,128)(2,1)} %bqkv_hbm.1, bf16[1024,4096]{1,0:T(8,128)(2,1)} %bitcast.13, ...), custom_call_target="tpu_custom_call" | custom-call | tf_op jit(solution)/shard_map/decoder_layer/pallas_call | solution.py:403
  56.7 0.7 %copy.15 = bf16[3,16,4096]{2,1,0:T(8,128)(2,1)} copy(bf16[3,16,4096]{2,1,0:T(8,128)(2,1)S(1)} %bitcast.11) | data formatting | bytes 786432

commit v6 on v5

--- a/solution.py
+++ b/solution.py
@@ -19,10 +19,12 @@
 QKV = 3 * HEADS * HEAD_DIM
 
 PK, PN = 1024, 512
+DIRECT = 256
 NK, NN = D // PK, D // PN
 AG1_CHUNKS = [(k * PK, PK) for k in range(NK)]
 AG2_CHUNKS = [(0, 1024), (1024, 512), (1536, 1024), (2560, 1024), (3584, 512)]
-RS_CHUNKS = [(n * PN, PN) for n in range(NN)]
+RS1_CHUNKS = [(DIRECT, PN - DIRECT)] + [(n * PN, PN) for n in range(1, NN)]
+RS2_CHUNKS = [(n * PN, PN) for n in range(NN)]
 RING = 9
 G_OUT, G_UP, G_DOWN, G_END = 6, 8, 16, 24
 STAGE_ROWS, STAGES = 256, 4
@@ -31,7 +33,7 @@
 
 def kernel(x_hbm, g1_hbm, b1_hbm, wqkv_hbm, bqkv_hbm, wout_hbm, bout_hbm, g2_hbm, b2_hbm, wup_hbm, bup_hbm, wdown_hbm, bdown_hbm, out_ref,
            stage, x_own, h_all, x1_all, h2_even, h2_odd, acc, qkv_bf, ctx, u,
-           psend1, prec1, xsend1, xrec1, psend2, prec2, xsend2, xrec2, stats, stat_cols, square,
+           dsend, drec, psend1, prec1, xsend1, xrec1, psend2, prec2, xsend2, xrec2, stats, stat_cols, square,
            vec_f32, vec_bf, bqkv_v, rows, bqkv_row, mask,
            stage_sem, ring_sem, small_sem, send_sem, gather_sem, st_sem, rs_sem, *ring):
     dp = lax.axis_index("dp")
@@ -43,7 +45,7 @@
     far = lax.rem(partner + 2, 4)
     other_core = 1 - core
     other_chip = 1 - chip
-    SEND_AG1, SEND_AG2, SEND_ST, SEND_RS1, SEND_RS2 = 0, 1, 2, 3, 5
+    SEND_AG1, SEND_AG2, SEND_ST, SEND_RS1, SEND_RS2, SEND_DIRECT = 0, 1, 2, 3, 5, 7
 
     def remote(src, dst, send, recv, peer):
         return pltpu.make_async_remote_copy(src_ref=src, dst_ref=dst, send_sem=send, recv_sem=recv, device_id=(dp, peer), device_id_type=MESH)
@@ -223,65 +225,84 @@
         for j, p in zip(heads, ps):
             ctx[:, j * HEAD_DIM:(j + 1) * HEAD_DIM] = jnp.dot(p, part_of(2, j), preferred_element_type=F32).astype(BF16)
 
-    def reduction(psend, prec, xsend, xrec, send):
+    def reduction(chunks, psend, prec, xsend, xrec, send):
         def pair(n):
-            at = (slice(None), slice(None), pl.ds(*RS_CHUNKS[n]))
+            at = (slice(None), slice(None), pl.ds(*chunks[n]))
             return remote(psend.at[at], prec.at[at], send_sem.at[send], rs_sem.at[0, n], partner)
 
         def across(n):
-            at = (slice(None), pl.ds(*RS_CHUNKS[n]))
+            at = (slice(None), pl.ds(*chunks[n]))
             return remote(xsend.at[at], xrec.at[at], send_sem.at[send + 1], rs_sem.at[1, n], cross)
 
-        def to_pair(n, part):
-            cols = pl.ds(*RS_CHUNKS[n])
-            acc[:, :, cols] = part.reshape(4, ROWS, RS_CHUNKS[n][1])
+        def to_pair(n):
+            cols = pl.ds(*chunks[n])
             for q in range(2):
                 psend[q, :, cols] = acc[2 * q + other_core, :, cols].astype(BF16)
             pair(n).start()
 
         def to_cross(n):
-            cols = pl.ds(*RS_CHUNKS[n])
+            cols = pl.ds(*chunks[n])
             pair(n).wait_recv()
             xsend[:, cols] = (acc[2 * other_chip + core, :, cols] + prec[other_chip, :, cols].astype(F32)).astype(BF16)
             across(n).start()
 
         def total(n):
-            cols = pl.ds(*RS_CHUNKS[n])
+            cols = pl.ds(*chunks[n])
             across(n).wait_recv()
             return acc[me, :, cols] + prec[chip, :, cols].astype(F32) + xrec[:, cols].astype(F32)
 
         def drain():
-            remote(psend, prec, send_sem.at[send], rs_sem.at[0, 0], partner).wait_send()
-            remote(xsend, xrec, send_sem.at[send + 1], rs_sem.at[1, 0], cross).wait_send()
+            rest = pl.ds(chunks[0][0], D - chunks[0][0])
+            at, sems = (slice(None), slice(None), rest), (send_sem.at[send], rs_sem.at[0, 0])
+            remote(psend.at[at], prec.at[at], *sems, partner).wait_send()
+            at, sems = (slice(None), rest), (send_sem.at[send + 1], rs_sem.at[1, 0])
+            remote(xsend.at[at], xrec.at[at], *sems, cross).wait_send()
 
         return to_pair, to_cross, total, drain
 
-    NR = len(RS_CHUNKS)
-    rs1_pair, rs1_cross, rs1_total, rs1_drain = reduction(psend1, prec1, xsend1, xrec1, SEND_RS1)
-    rs2_pair, rs2_cross, rs2_total, rs2_drain = reduction(psend2, prec2, xsend2, xrec2, SEND_RS2)
+    NR = len(RS1_CHUNKS)
+    rs1_pair, rs1_cross, rs1_total, rs1_drain = reduction(RS1_CHUNKS, psend1, prec1, xsend1, xrec1, SEND_RS1)
+    rs2_pair, rs2_cross, rs2_total, rs2_drain = reduction(RS2_CHUNKS, psend2, prec2, xsend2, xrec2, SEND_RS2)
 
     def ag2(which, block, peer, c):
         return push(x1_all, AG2_CHUNKS, SEND_AG2, which, block, peer, c)
 
     def st(block, peer):
         return remote(stats.at[block], stats.at[block], send_sem.at[SEND_ST], st_sem.at[0], peer)
+
+    def direct(i):
+        return remote(dsend.at[i], drec.at[i], send_sem.at[SEND_DIRECT], rs_sem.at[0, NR], (cross, far, partner)[i])
+
+    def direct_total():
+        remote(dsend, drec, send_sem.at[SEND_DIRECT], rs_sem.at[0, NR], cross).wait_recv()
+        total = acc[me, :, 0:DIRECT]
+        for i in (2, 0, 1):
+            total = total + drec[i].astype(F32)
+        return total
 
     ctx_rows = ctx[...]
     lead = 2
     for g in range(G_OUT, G_UP):
         await_group(g)
-    for n, (start, size) in enumerate(RS_CHUNKS):
-        g, m = G_OUT + start // PN // 4, start // PN % 4
-        rs1_pair(n, jnp.dot(ctx_rows, ring[g % RING][m, :, start % PN:start % PN + size], preferred_element_type=F32))
+    for n in range(NR):
+        part = jnp.dot(ctx_rows, ring[(G_OUT + n // 4) % RING][n % 4], preferred_element_type=F32)
+        acc[:, :, n * PN:(n + 1) * PN] = part.reshape(4, ROWS, PN)
+        if n == 0:
+            for i, peer in enumerate((cross, far, partner)):
+                dsend[i] = acc[peer, :, 0:DIRECT].astype(BF16)
+            for i in range(3):
+                direct(i).start()
+        rs1_pair(n)
         if n >= lead:
             rs1_cross(n - lead)
     for g in range(G_OUT, G_UP):
         load_group(g + RING)
     for n in range(NR - lead, NR):
         rs1_cross(n)
-    for n, (start, size) in enumerate(RS_CHUNKS):
+    for n, (start, size) in enumerate([(0, DIRECT)] + RS1_CHUNKS):
         cols = pl.ds(start, size)
-        x1 = (x_own[:, cols].astype(F32) + (rs1_total(n) + rows[BOUT, :, cols])).astype(BF16)
+        total = rs1_total(n - 1) if n else direct_total()
+        x1 = (x_own[:, cols].astype(F32) + (total + rows[BOUT, :, cols])).astype(BF16)
         x1_all[me, :, cols] = x1
         x1 = x1.astype(F32)
         part_mean = jnp.mean(x1, axis=-1, keepdims=True)
@@ -326,13 +347,13 @@
         edges = sorted({start, start + size} | {k * PK for k in range(NK) if start < k * PK < start + size})
         return [(lo // PK, lo % PK, hi - lo) for lo, hi in zip(edges, edges[1:])]
 
-    def up_half(c, half):
+    def up_panels(c, panels):
         h = all_rows((h2_even, h2_odd)[c % 2], 0, AG2_CHUNKS[c][1])
-        for n in range(half * 4, half * 4 + 4):
+        for n in panels:
             part, done = all_rows(acc, n * PN, PN) if c else rows[BUP, :, n * PN:(n + 1) * PN], 0
             total = None
             for k, row, size in blocks_of(c):
-                term = jnp.dot(h[:, done:done + size], ring[(G_UP + k * 2 + half) % RING][n % 4, row:row + size, :], preferred_element_type=F32)
+                term = jnp.dot(h[:, done:done + size], ring[(G_UP + k * 2 + n // 4) % RING][n % 4, row:row + size, :], preferred_element_type=F32)
                 total, done = term if total is None else total + term, done + size
             part = total + part
             if c < len(AG2_CHUNKS) - 1:
@@ -346,6 +367,10 @@
             term = jnp.dot(u[:, k * PK:(k + 1) * PK], ring[(G_DOWN + n) % RING][k], preferred_element_type=F32)
             total = term if total is None else total + term
         return total
+
+    def down_to_pair(n):
+        acc[:, :, n * PN:(n + 1) * PN] = down_sum(n).reshape(4, ROWS, PN)
+        rs2_pair(n)
 
     ag2_forward(0)
     remote(stats.at[pl.ds(0, 3)], stats.at[pl.ds(0, 3)], send_sem.at[SEND_ST], st_sem.at[0], partner).wait_recv()
@@ -360,11 +385,12 @@
             if row == 0:
                 await_group(G_UP + 2 * k)
                 await_group(G_UP + 2 * k + 1)
-        up_half(c, 0)
+        before = (3, 5, 4, 0)[c]
+        up_panels(c, range(before))
         ag2_forward(c + 1)
         ag2(PARTNER, partner, partner, c + 1).wait_recv()
         normalize(c + 1, (me, partner, cross))
-        up_half(c, 1)
+        up_panels(c, range(before, NN))
         for k, row, size in blocks_of(c):
             if row + size == PK:
                 load_group(G_UP + 2 * k + RING)
@@ -373,23 +399,23 @@
         normalize(c + 1, (far,))
 
     await_group(G_DOWN)
-    for half in range(2):
-        up_half(len(AG2_CHUNKS) - 1, half)
-    rs2_pair(0, down_sum(0))
+    up_panels(len(AG2_CHUNKS) - 1, range(NN))
+    down_to_pair(0)
     load_group(G_DOWN - 2 + RING)
     load_group(G_DOWN - 1 + RING)
     for n in range(1, NR):
         await_group(G_DOWN + n)
-        rs2_pair(n, down_sum(n))
+        down_to_pair(n)
         rs2_cross(n - 1)
     rs2_cross(NR - 1)
-    for n, (start, size) in enumerate(RS_CHUNKS):
+    for n, (start, size) in enumerate(RS2_CHUNKS):
         cols = pl.ds(start, size)
         out_ref[:, cols] = (x1_all[me, :, cols].astype(F32) + (rs2_total(n) + rows[BDOWN, :, cols])).astype(BF16)
 
     for buf, send in ((h_all, SEND_AG1), (x1_all, SEND_AG2), (stats, SEND_ST)):
         remote(buf.at[pl.ds(0, 3)], buf.at[pl.ds(0, 3)], send_sem.at[send], st_sem.at[0], partner).wait_send()
     rs1_drain()
+    remote(dsend, drec, send_sem.at[SEND_DIRECT], rs_sem.at[0, NR], cross).wait_send()
     rs2_drain()
 
 
@@ -416,6 +442,8 @@
                 pltpu.VMEM((TOKENS, QKV), BF16),
                 pltpu.VMEM((TOKENS, HEADS * HEAD_DIM), BF16),
                 pltpu.VMEM((TOKENS, FF), BF16),
+                pltpu.VMEM((3, ROWS, DIRECT), BF16),
+                pltpu.VMEM((3, ROWS, DIRECT), BF16),
                 *rs_buffers,
                 *rs_buffers,
                 pltpu.VMEM((4, 8, 128), F32),
@@ -427,7 +455,7 @@
                 pltpu.VMEM((7, 1, D), F32),
                 pltpu.VMEM((1, QKV), F32),
                 pltpu.VMEM((TOKENS, TOKENS), F32),
-                dma((STAGES,)), dma((RING,)), dma((5,)), dma((7,)), dma((3, len(AG2_CHUNKS))), dma((1,)), dma((2, len(RS_CHUNKS))),
+                dma((STAGES,)), dma((RING,)), dma((5,)), dma((8,)), dma((3, len(AG2_CHUNKS))), dma((1,)), dma((2, NN + 1)),
                 *[pltpu.VMEM((4, PK, PN), BF16)] * RING,
             ],
             compiler_params=pltpu.CompilerParams(collective_id=0, has_side_effects=True, vmem_limit_bytes=62 * 2**20),

time: 57.6 us -> 56.7 us (0.984)
  Pallas kernels: 56.7 us -> 55.8 us
    pallas_call x1, Pallas kernels: 56.7 us -> 55.8 us  [device_body(): pl.pallas_call(kernel, out_shape=pltpu.VMEM((ROWS, D), BF16), in_specs=[h...]
where the time goes in v6:
time: 56.7 us; the launch traced here: 56.6 us
  Pallas kernels  55.8 us (98%)
  local copies, waits for them, and re-layouts  0.75 us (1%)
    pallas_call x1, Pallas kernels, device_body(): pl.pallas_call(kernel, out_shape=pltpu.VMEM((ROWS, D), BF16), in_specs=[h...  55.8 us

profile of v6, /device:TPU:0, one launch (start us, length us, event | category | flops | bytes accessed | tf_op | source)
XLA Modules:
  0.0 56.6 jit_solution(4726264450167407113)
XLA Ops:
  0.0 55.8 %decoder_layer.1 = bf16[48,4096]{1,0:T(8,128)(2,1)S(1)} custom-call(bf16[48,4096]{1,0:T(8,128)(2,1)} %bitcast.14, f32[32,128]{1,0:T(8,128)} %bitcast.15, f32[32,128]{1,0:T(8,128)} %bitcast.16, bf16[4096,3,8,128]{3,2,1,0:T(8,128)(2,1)} %wqkv_hbm.1, bf16[3,8,128]{2,1,0:T(8,128)(2,1)} %bqkv_hbm.1, bf16[1024,4096]{1,0:T(8,128)(2,1)} %bitcast.13, ...), custom_call_target="tpu_custom_call" | custom-call | tf_op jit(solution)/shard_map/decoder_layer/pallas_call | solution.py:429
  55.8 0.7 %copy.15 = bf16[3,16,4096]{2,1,0:T(8,128)(2,1)} copy(bf16[3,16,4096]{2,1,0:T(8,128)(2,1)S(1)} %bitcast.11) | data formatting | bytes 786432

commit v7 on v6

--- a/solution.py
+++ b/solution.py
@@ -176,7 +176,7 @@
 
     (q_seq, q_pos), (k_seq, k_pos) = token_place(0), token_place(1)
     square[...] = jnp.zeros_like(square)
-    mask[...] = ((q_seq == k_seq) & (q_pos >= k_pos)).astype(F32)
+    mask[...] = jnp.where(q_seq == k_seq, jnp.where(q_pos >= k_pos, 0.0, -1e30), -jnp.inf).astype(F32)
     ag1_forward(0)
     ag1_forward(1)
     relayout_chunk(3)
@@ -185,11 +185,30 @@
     def all_rows(ref, start, size):
         return ref[:, :, start:start + size].reshape(TOKENS, size)
 
+    def part_of(t, j):
+        return qkv_bf[:, (t * HEADS + j) * HEAD_DIM:(t * HEADS + j + 1) * HEAD_DIM]
+
+    def scores(heads):
+        return [lax.dot_general(part_of(0, j), part_of(1, j), (((1,), (1,)), ((), ())), preferred_element_type=F32) for j in heads]
+
+    def softmax(logits):
+        fill = mask[...]
+        logits = [jnp.where(fill == 0.0, x * HEAD_DIM ** -0.5, fill) for x in logits]
+        tops = [jnp.max(x, axis=-1, keepdims=True) for x in logits]
+        es = [jnp.exp(x - t) for x, t in zip(logits, tops)]
+        sums = [jnp.sum(e, axis=-1, keepdims=True) for e in es]
+        return [(e * (1.0 / z)).astype(BF16) for e, z in zip(es, sums)]
+
+    def weigh(heads, ps):
+        for j, p in zip(heads, ps):
+            ctx[:, j * HEAD_DIM:(j + 1) * HEAD_DIM] = jnp.dot(p, part_of(2, j), preferred_element_type=F32).astype(BF16)
+
     def qkv_block(chunks):
         for c in chunks:
             ag1(FAR, far, partner, c).wait_recv()
         first, last = chunks[0] == 0, chunks[-1] == NK - 1
-        for n in range(6):
+        early = None
+        for n in (0, 2, 4, 1, 3, 5):
             part = None if first else all_rows(acc, n * PN, PN)
             for c in chunks:
                 p = c * 6 + n
@@ -197,6 +216,12 @@
                 part = term if part is None else part + term
             if last:
                 qkv_bf[:, n * PN:(n + 1) * PN] = (part + bqkv_row[:, n * PN:(n + 1) * PN]).astype(BF16)
+                if n == 4:
+                    early = scores(range(4))
+                if n in (1, 3):
+                    half = softmax(early[:2])
+                    early = early[2:]
+                    weigh(range(n - 1, n + 1), half)
             else:
                 acc[:, :, n * PN:(n + 1) * PN] = part.reshape(4, ROWS, PN)
         for g in range(chunks[0] * 6 // 4, (chunks[-1] + 1) * 6 // 4):
@@ -209,21 +234,8 @@
     qkv_block((1,))
     qkv_block((2, 3))
 
-    keep = mask[...] > 0.5
-    for first in range(0, HEADS, 4):
-        heads = range(first, first + 4)
-
-        def part_of(t, j):
-            return qkv_bf[:, (t * HEADS + j) * HEAD_DIM:(t * HEADS + j + 1) * HEAD_DIM]
-
-        logits = [lax.dot_general(part_of(0, j), part_of(1, j), (((1,), (1,)), ((), ())), preferred_element_type=F32) for j in heads]
-        logits = [jnp.where(keep, x * HEAD_DIM ** -0.5, -1e30) for x in logits]
-        tops = [jnp.max(x, axis=-1, keepdims=True) for x in logits]
-        es = [jnp.exp(x - t) for x, t in zip(logits, tops)]
-        sums = [jnp.sum(e, axis=-1, keepdims=True) for e in es]
-        ps = [(e * (1.0 / z)).astype(BF16) for e, z in zip(es, sums)]
-        for j, p in zip(heads, ps):
-            ctx[:, j * HEAD_DIM:(j + 1) * HEAD_DIM] = jnp.dot(p, part_of(2, j), preferred_element_type=F32).astype(BF16)
+    ps = softmax(scores(range(4, 8)))
+    weigh(range(4, 8), ps)
 
     def reduction(chunks, psend, prec, xsend, xrec, send):
         def pair(n):
@@ -267,8 +279,8 @@
     def ag2(which, block, peer, c):
         return push(x1_all, AG2_CHUNKS, SEND_AG2, which, block, peer, c)
 
-    def st(block, peer):
-        return remote(stats.at[block], stats.at[block], send_sem.at[SEND_ST], st_sem.at[0], peer)
+    def st(block, peer, sem):
+        return remote(stats.at[block], stats.at[block], send_sem.at[SEND_ST], st_sem.at[sem], peer)
 
     def direct(i):
         return remote(dsend.at[i], drec.at[i], send_sem.at[SEND_DIRECT], rs_sem.at[0, NR], (cross, far, partner)[i])
@@ -319,8 +331,9 @@
     lane = lax.broadcasted_iota(jnp.int32, (ROWS, 128), 1)
     square[0:ROWS, :] = jnp.where(lane == 0, mean, lax.rsqrt(dist * (1.0 / D) + LN_EPS))
     stats[me] = square[...].T[:8]
-    for peer in (cross, far, partner):
-        st(me, peer).start()
+    for peer in (cross, far):
+        st(me, peer, 1).start()
+    st(me, partner, 0).start()
     for c in range(1, len(AG2_CHUNKS)):
         ag2(CROSS, me, cross, c).start()
         ag2(PARTNER, me, partner, c).start()
@@ -372,14 +385,21 @@
         acc[:, :, n * PN:(n + 1) * PN] = down_sum(n).reshape(4, ROWS, PN)
         rs2_pair(n)
 
-    ag2_forward(0)
-    remote(stats.at[pl.ds(0, 3)], stats.at[pl.ds(0, 3)], send_sem.at[SEND_ST], st_sem.at[0], partner).wait_recv()
-    for d in range(4):
+    def columns(d):
         square[0:8, :] = stats[d]
         stat_cols[d] = square[...].T[:ROWS]
+
+    st(partner, partner, 0).wait_recv()
+    columns(me)
+    columns(partner)
     ag2(PARTNER, partner, partner, 0).wait_recv()
+    normalize(0, (me, partner))
+    ag2_forward(0)
+    remote(stats.at[pl.ds(0, 2)], stats.at[pl.ds(0, 2)], send_sem.at[SEND_ST], st_sem.at[1], cross).wait_recv()
+    columns(cross)
+    columns(far)
     ag2(FAR, far, partner, 0).wait_recv()
-    normalize(0, range(4))
+    normalize(0, (cross, far))
     for c in range(len(AG2_CHUNKS) - 1):
         for k, row, size in blocks_of(c):
             if row == 0:
@@ -455,7 +475,7 @@
                 pltpu.VMEM((7, 1, D), F32),
                 pltpu.VMEM((1, QKV), F32),
                 pltpu.VMEM((TOKENS, TOKENS), F32),
-                dma((STAGES,)), dma((RING,)), dma((5,)), dma((8,)), dma((3, len(AG2_CHUNKS))), dma((1,)), dma((2, NN + 1)),
+                dma((STAGES,)), dma((RING,)), dma((5,)), dma((8,)), dma((3, len(AG2_CHUNKS))), dma((2,)), dma((2, NN + 1)),
                 *[pltpu.VMEM((4, PK, PN), BF16)] * RING,
             ],
             compiler_params=pltpu.CompilerParams(collective_id=0, has_side_effects=True, vmem_limit_bytes=62 * 2**20),

time: 56.7 us -> 56.6 us (level)
  no operation moved by 1% of the time
where the time goes in v7:
time: 56.6 us; the launch traced here: 56.5 us
  Pallas kernels  55.7 us (98%)
  local copies, waits for them, and re-layouts  0.75 us (1%)
    pallas_call x1, Pallas kernels, device_body(): pl.pallas_call(kernel, out_shape=pltpu.VMEM((ROWS, D), BF16), in_specs=[h...  55.7 us

profile of v7, /device:TPU:0, one launch (start us, length us, event | category | flops | bytes accessed | tf_op | source)
XLA Modules:
  0.0 56.5 jit_solution(94765572759710295)
XLA Ops:
  0.0 55.7 %decoder_layer.1 = bf16[48,4096]{1,0:T(8,128)(2,1)S(1)} custom-call(bf16[48,4096]{1,0:T(8,128)(2,1)} %bitcast.14, f32[32,128]{1,0:T(8,128)} %bitcast.15, f32[32,128]{1,0:T(8,128)} %bitcast.16, bf16[4096,3,8,128]{3,2,1,0:T(8,128)(2,1)} %wqkv_hbm.1, bf16[3,8,128]{2,1,0:T(8,128)(2,1)} %bqkv_hbm.1, bf16[1024,4096]{1,0:T(8,128)(2,1)} %bitcast.13, ...), custom_call_target="tpu_custom_call" | custom-call | tf_op jit(solution)/shard_map/decoder_layer/pallas_call | solution.py:449
  55.7 0.7 %copy.15 = bf16[3,16,4096]{2,1,0:T(8,128)(2,1)} copy(bf16[3,16,4096]{2,1,0:T(8,128)(2,1)S(1)} %bitcast.11) | data formatting | bytes 786432

commit v8 on v7

--- a/solution.py
+++ b/solution.py
@@ -35,7 +35,7 @@
            stage, x_own, h_all, x1_all, h2_even, h2_odd, acc, qkv_bf, ctx, u,
            dsend, drec, psend1, prec1, xsend1, xrec1, psend2, prec2, xsend2, xrec2, stats, stat_cols, square,
            vec_f32, vec_bf, bqkv_v, rows, bqkv_row, mask,
-           stage_sem, ring_sem, small_sem, send_sem, gather_sem, st_sem, rs_sem, *ring):
+           ring_sem, send_sem, gather_sem, st_sem, rs_sem, *ring):
     dp = lax.axis_index("dp")
     me = lax.axis_index("tp")
     core = lax.rem(me, 2)
@@ -51,7 +51,7 @@
         return pltpu.make_async_remote_copy(src_ref=src, dst_ref=dst, send_sem=send, recv_sem=recv, device_id=(dp, peer), device_id_type=MESH)
 
     def stage_copy(i):
-        return pltpu.make_async_copy(wqkv_hbm.at[pl.ds(i * STAGE_ROWS, STAGE_ROWS)], stage.at[lax.rem(i, STAGES)], stage_sem.at[lax.rem(i, STAGES)])
+        return pltpu.make_async_copy(wqkv_hbm.at[pl.ds(i * STAGE_ROWS, STAGE_ROWS)], stage.at[lax.rem(i, STAGES)], rs_sem.at[0, 4 + lax.rem(i, STAGES)])
 
     def load_group(g):
         to, sem = ring[g % RING], ring_sem.at[g % RING]
@@ -75,10 +75,10 @@
     for peer in (partner, cross, far):
         pl.semaphore_signal(barrier, inc=1, device_id=(dp, peer), device_id_type=MESH)
     G1, B1, G2, B2, BOUT, BUP, BDOWN = range(7)
-    x_copy = pltpu.make_async_copy(x_hbm, x_own, small_sem.at[4])
+    x_copy = pltpu.make_async_copy(x_hbm, x_own, st_sem.at[0])
+    x_copy.start()
     for i, src in enumerate((g1_hbm, b1_hbm)):
-        pltpu.make_async_copy(src, vec_f32.at[i], small_sem.at[0]).start()
-    x_copy.start()
+        pltpu.make_async_copy(src, vec_f32.at[i], rs_sem.at[0, 0]).start()
     stage_copy(0).start()
 
     def f32_row(i):
@@ -91,7 +91,7 @@
         var = jnp.mean(centered * centered, axis=-1, keepdims=True)
         return mean, lax.rsqrt(var + LN_EPS)
 
-    pltpu.make_async_copy(vec_f32.at[pl.ds(2, 2)], vec_f32.at[pl.ds(0, 2)], small_sem.at[0]).wait()
+    pltpu.make_async_copy(vec_f32.at[pl.ds(2, 2)], vec_f32.at[pl.ds(0, 2)], rs_sem.at[0, 0]).wait()
     for i in (G1, B1):
         f32_row(i)
     stage_copy(1).start()
@@ -99,10 +99,10 @@
     for i in range(2, STAGES):
         stage_copy(i).start()
     for i, src in enumerate((g2_hbm, b2_hbm)):
-        pltpu.make_async_copy(src, vec_f32.at[2 + i], small_sem.at[1]).start()
+        pltpu.make_async_copy(src, vec_f32.at[2 + i], rs_sem.at[0, 1]).start()
     for i, src in enumerate((bout_hbm, bup_hbm, bdown_hbm)):
-        pltpu.make_async_copy(src, vec_bf.at[i], small_sem.at[2]).start()
-    bqkv_copy = pltpu.make_async_copy(bqkv_hbm, bqkv_v, small_sem.at[3])
+        pltpu.make_async_copy(src, vec_bf.at[i], rs_sem.at[0, 2]).start()
+    bqkv_copy = pltpu.make_async_copy(bqkv_hbm, bqkv_v, rs_sem.at[0, 3])
     bqkv_copy.start()
     for b in range(N_BATCH):
         r = pl.ds(b * BLOCK, BLOCK)
@@ -153,8 +153,8 @@
 
     for k in range(3):
         relayout_chunk(k)
-    pltpu.make_async_copy(vec_f32.at[pl.ds(0, 2)], vec_f32.at[pl.ds(2, 2)], small_sem.at[1]).wait()
-    pltpu.make_async_copy(vec_bf, vec_bf, small_sem.at[2]).wait()
+    pltpu.make_async_copy(vec_f32.at[pl.ds(0, 2)], vec_f32.at[pl.ds(2, 2)], rs_sem.at[0, 1]).wait()
+    pltpu.make_async_copy(vec_bf, vec_bf, rs_sem.at[0, 2]).wait()
     bqkv_copy.wait()
     for i in (G2, B2):
         f32_row(i)
@@ -475,7 +475,7 @@
                 pltpu.VMEM((7, 1, D), F32),
                 pltpu.VMEM((1, QKV), F32),
                 pltpu.VMEM((TOKENS, TOKENS), F32),
-                dma((STAGES,)), dma((RING,)), dma((5,)), dma((8,)), dma((3, len(AG2_CHUNKS))), dma((2,)), dma((2, NN + 1)),
+                dma((RING,)), dma((8,)), dma((3, len(AG2_CHUNKS))), dma((2,)), dma((2, NN + 1)),
                 *[pltpu.VMEM((4, PK, PN), BF16)] * RING,
             ],
             compiler_params=pltpu.CompilerParams(collective_id=0, has_side_effects=True, vmem_limit_bytes=62 * 2**20),

time: 56.6 us -> 56.5 us (level)
  no operation moved by 1% of the time
where the time goes in v8:
time: 56.5 us; the launch traced here: 56.4 us
  Pallas kernels  55.6 us (98%)
  local copies, waits for them, and re-layouts  0.75 us (1%)
    pallas_call x1, Pallas kernels, device_body(): pl.pallas_call(kernel, out_shape=pltpu.VMEM((ROWS, D), BF16), in_specs=[h...  55.6 us

profile of v8, /device:TPU:0, one launch (start us, length us, event | category | flops | bytes accessed | tf_op | source)
XLA Modules:
  0.0 56.4 jit_solution(1133645040524546768)
XLA Ops:
  0.0 55.6 %decoder_layer.1 = bf16[48,4096]{1,0:T(8,128)(2,1)S(1)} custom-call(bf16[48,4096]{1,0:T(8,128)(2,1)} %bitcast.14, f32[32,128]{1,0:T(8,128)} %bitcast.15, f32[32,128]{1,0:T(8,128)} %bitcast.16, bf16[4096,3,8,128]{3,2,1,0:T(8,128)(2,1)} %wqkv_hbm.1, bf16[3,8,128]{2,1,0:T(8,128)(2,1)} %bqkv_hbm.1, bf16[1024,4096]{1,0:T(8,128)(2,1)} %bitcast.13, ...), custom_call_target="tpu_custom_call" | custom-call | tf_op jit(solution)/shard_map/decoder_layer/pallas_call | solution.py:449
  55.6 0.7 %copy.15 = bf16[3,16,4096]{2,1,0:T(8,128)(2,1)} copy(bf16[3,16,4096]{2,1,0:T(8,128)(2,1)S(1)} %bitcast.11) | data formatting | bytes 786432
